TPU v7x, 512 devices: a whole 4x8x8 slice. The times are simulated.
512 devices in a mesh: dp: 64 (over x, z_lo, y), tensor: 8 (over z_hi, core).
Axes of the slice: x: 4, y: 8, z: 8 (z_hi: 4, z_lo: 2; z = z_hi * 2 + z_lo), core: 2. Of those that a mesh axis runs over, the one named last changes fastest.
Arguments:
- layer_input: bfloat16 [2560, 5120], P('dp', 'tensor'), may hold values from -6 to 6
- up_weight: bfloat16 [5120, 13824], P('dp', 'tensor'), may hold values from -0.078125 to 0.078125
- grad_output: bfloat16 [2560, 13824], P('dp', 'tensor'), may hold values from -60 to 60
- factor_input: float32 [5120, 5120], P('dp', 'tensor'), may hold values from -4 to 15, as said below
- factor_grad: float32 [13824, 13824], P('dp', 'tensor'), may hold values from -4 to 15, as said below
- decay: float32 [1], replicated, may hold values from 0.5 to 0.95
Outputs:
- grad_weight: float32 [5120, 13824], P('dp', 'tensor')
- grad_input: bfloat16 [2560, 5120], P('tensor', 'dp')
- new_factor_input: float32 [5120, 5120], P('dp', 'tensor')
- new_factor_grad: float32 [13824, 13824], P('dp', 'tensor')
Inputs may be any that keep to these rules, and one draw needn't show every extreme that they name: `factor_input`: symmetric. `factor_grad`: symmetric.
All inputs are finite; a program needn't handle non-finite values.
Results may differ from a plain program's by a relative error of at most 0.001.
Values may be sent and summed in bfloat16 or wider, within the bound.
No kernel may reach another device: no remote copies, remote signals or barrier semaphores. Data moves between devices by JAX's collectives and lax.ppermute only.
A program may use at most 128 MiB of HBM per device.

v0:
```python
import jax
import jax.numpy as jnp
from jax import lax
from jax.sharding import Mesh
from jax.sharding import PartitionSpec as P

DP = ("dp_0", "dp_1", "dp_2")
TENSOR = ("tensor_0", "tensor_1")


def laid_out(parts, dim):
    lengths = list(parts.shape[1:])
    lengths[dim] *= parts.shape[0]
    return jnp.moveaxis(parts, 0, dim).reshape(lengths)


def all_blocks(x, axes, sequence):
    parts = x[None]
    for k in sequence:
        parts = lax.all_gather(parts, axes[k], axis=0, tiled=True)
    held = [lax.axis_size(axes[k]) for k in reversed(sequence)]
    parts = parts.reshape(*held, *x.shape)
    turned = sorted(range(len(sequence)), key=lambda place: sequence[len(sequence) - 1 - place])
    return parts.transpose(*turned, *range(len(sequence), parts.ndim)).reshape(-1, *x.shape)


def whole_of(x, axes, sequence, dim):
    return laid_out(all_blocks(x, axes, sequence), dim)


def picked(x, axis, root):
    return lax.dynamic_index_in_dim(lax.all_gather(x, axis), root, 0, keepdims=False)


def broadcast_by_axis(x, axes, root):
    x = jnp.where(lax.axis_index(axes) == root, x, jnp.zeros_like(x))
    for axis in axes:
        x = lax.psum(x, axis)
    return x


def contract_rows(left, right):
    return lax.dot_general(
        left, right, (((0,), (0,)), ((), ())), preferred_element_type=jnp.float32
    )


def contract_cols(left, right):
    return lax.dot_general(
        left, right, (((1,), (1,)), ((), ())), preferred_element_type=jnp.float32
    )


def local(layer_input, up_weight, grad_output, factor_input, factor_grad, decay):
    ratio = lax.axis_size(DP) // lax.axis_size(TENSOR)
    own = lax.axis_index(DP)
    owner = own // ratio
    token_total = layer_input.shape[0] * lax.axis_size(DP)
    keep = decay[0]
    blend = (1.0 - keep) / token_total
    feat_rows = up_weight.shape[0]
    unit_rows = factor_grad.shape[0]
    local_rows = grad_output.shape[0]
    input_all = whole_of(layer_input, DP, (1, 0, 2), 0)
    input_slice = lax.dynamic_slice_in_dim(input_all, own % ratio * feat_rows, feat_rows, 1)
    input_part = picked(input_slice, TENSOR, owner)
    gram_input = contract_rows(input_part, input_all)
    new_factor_input = keep * factor_input + blend * gram_input
    blocks = grad_output.reshape(local_rows, ratio, unit_rows)
    spread = jnp.tile(blocks, (1, lax.axis_size(TENSOR), 1))
    received = lax.all_to_all(spread, DP, split_axis=1, concat_axis=0, tiled=True)
    grad_part = broadcast_by_axis(received.reshape(token_total, unit_rows), TENSOR, owner)
    piece = whole_of(grad_output, DP, (1, 0, 2), 0)
    weight_sum = contract_rows(input_part, piece)
    gram_sum = contract_rows(grad_part, piece)
    partial_value = contract_cols(piece, up_weight)
    new_factor_grad = keep * factor_grad + blend * gram_sum
    grad_input = lax.psum_scatter(partial_value, TENSOR, scatter_dimension=0, tiled=True).astype(
        jnp.bfloat16
    )
    return (weight_sum, grad_input, new_factor_input, new_factor_grad)


def solution(mesh):
    finer = Mesh(
        mesh.devices.reshape(4, 2, 8, 4, 2), ("dp_0", "dp_1", "dp_2", "tensor_0", "tensor_1")
    )
    return jax.shard_map(
        local,
        mesh=finer,
        in_specs=(P(DP, TENSOR), P(DP, TENSOR), P(DP, TENSOR), P(DP, TENSOR), P(DP, TENSOR), P()),
        out_specs=(P(DP, TENSOR), P(TENSOR, DP), P(DP, TENSOR), P(DP, TENSOR)),
        check_vma=False,
    )
```

profile of v0, /device:TPU:6, one launch (start us, length us, event | category | flops | bytes accessed | tf_op | source)
XLA Modules:
  0.0 331.8 jit_solution(1561070554311107136)
XLA Ops:
  8.0 0.0 copy-start
  8.0 0.0 copy-start.3
  8.0 0.0 all-gather.10.cloned.1.call-start
  8.1 8.8 %all-gather.2 = bf16[80,1728]{1,0:T(8,128)(2,1)} all-gather(bf16[40,1728]{1,0:T(8,128)(2,1)} %param.8), channel_id=4, replica_groups=mesh['dp_0'=4,'dp_1'=2,'dp_2'=8,'tensor_0'=4,'tensor_1'=2] {'dp_1'}, dimensions={0}, use_global_device_ids=true | all-gather | bytes 414720 | tf_op jit(solution)/shard_map/all_gather | solution.py:20
  16.9 0.0 all-gather.10.cloned.1.call-update
  16.9 0.0 all-gather.8.cloned.1.call-start
  16.9 5.0 %all-gather = bf16[80,640]{1,0:T(8,128)(2,1)S(1)} all-gather(bf16[40,640]{1,0:T(8,128)(2,1)} %param.6), channel_id=2, replica_groups=mesh['dp_0'=4,'dp_1'=2,'dp_2'=8,'tensor_0'=4,'tensor_1'=2] {'dp_1'}, dimensions={0}, use_global_device_ids=true | all-gather | bytes 153600 | tf_op jit(solution)/shard_map/all_gather | solution.py:20
  21.9 13.8 %all_gather.25 = bf16[8,40,640]{2,1,0:T(8,128)(2,1)} all-gather(bf16[2,40,640]{2,1,0:T(8,128)(2,1)S(1)} %bitcast.42), channel_id=1, replica_groups=mesh['dp_0'=4,'dp_1'=2,'dp_2'=8,'tensor_0'=4,'tensor_1'=2] {'dp_0'}, dimensions={0}, use_global_device_ids=true | all-gather | bytes 512000 | tf_op jit(solution)/shard_map/all_gather | solution.py:20
  35.8 0.0 all-gather.8.cloned.1.call-update
  35.8 0.0 copy-done.3
  35.8 0.2 tile.10
  36.1 1.1 tile.11
  37.3 10.0 %all-to-all-start = ((bf16[40,64,216]{2,0,1:T(8,128)(2,1)}), bf16[40,64,216]{2,0,1:T(8,128)(2,1)S(1)}, u32[]{:S(2)}, u32[]{:S(2)}) async-start(bf16[40,64,216]{2,0,1:T(8,128)(2,1)} %bitcast.11), calls=%async_computation | async-start | bytes 2621440 | tf_op jit(solution)/shard_map/all_to_all | solution.py:71
  47.2 0.0 all-reduce.3.cloned.1.call-start
  47.3 28.4 %all-to-all-done = bf16[40,64,216]{2,0,1:T(8,128)(2,1)S(1)} async-done(((bf16[40,64,216]{2,0,1:T(8,128)(2,1)}), bf16[40,64,216]{2,0,1:T(8,128)(2,1)S(1)}, u32[]{:S(2)}, u32[]{:S(2)}) %all-to-all-start) | async-done | bytes 1105952 | tf_op jit(solution)/shard_map/all_to_all | solution.py:71
  75.7 1.1 broadcast_select_fusion
  76.8 0.0 all-reduce.3.cloned.1.call-update
  76.9 0.0 all-gather.12.cloned.1.call-start
  76.9 0.0 all-gather.10.cloned.1.call-done
  76.9 0.7 all-gather.12.cloned.1.call-update
  77.6 0.0 all-gather.14.cloned.1.call-start
  77.7 28.0 %all-gather.8.cloned.1.call-done = bf16[64,40,640]{2,1,0:T(8,128)(2,1)} async-done(((bf16[8,40,640]{2,1,0:T(8,128)(2,1)}), bf16[64,40,640]{2,1,0:T(8,128)(2,1)}) %all-gather.8.cloned.1.call-update) | async-done | bytes 3276816 | tf_op jit(solution)/shard_map/all_gather | solution.py:20
  105.7 2.4 copy.14
  108.0 0.0 copy-start.1
  108.1 1.7 copy-done.1
  109.8 1.2 constant_dynamic-slice_fusion
  111.0 0.0 all-gather.14.cloned.1.call-update
  111.0 0.0 all-reduce.5.cloned.1.call-start
  111.0 52.4 %all-reduce.3.cloned.1.call-done = bf16[2560,216]{1,0:T(8,128)(2,1)} async-done(((bf16[2560,216]{1,0:T(8,128)(2,1)}), bf16[2560,216]{1,0:T(8,128)(2,1)}) %all-reduce.3.cloned.1.call-update) | async-done | bytes 1105936 | tf_op jit(solution)/shard_map/psum | solution.py:38
  163.5 0.0 all-reduce.5.cloned.1.call-update
  163.5 0.0 reduce-scatter.4.cloned.1.call-start
  164.2 48.2 %all-gather.12.cloned.1.call-done = bf16[64,40,1728]{2,1,0:T(8,128)(2,1)} async-done(((bf16[8,40,1728]{2,1,0:T(8,128)(2,1)}), bf16[64,40,1728]{2,1,0:T(8,128)(2,1)}) %all-gather.12.cloned.1.call-update) | async-done | bytes 8847376 | tf_op jit(solution)/shard_map/all_gather | solution.py:20
  212.4 7.8 %copy.15 = bf16[4,2,8,40,1728]{4,3,2,1,0:T(8,128)(2,1)} copy(bf16[4,2,8,40,1728]{4,3,1,0,2:T(8,128)(2,1)} %bitcast.38) | data formatting | bytes 17694720 | tf_op jit(solution)/shard_map/transpose | solution.py:24
  220.2 0.0 copy-done
  220.2 0.0 copy-start.4
  220.2 7.3 %fusion.9 = f32[2560,80]{1,0:T(8,128)} fusion(bf16[2560,1728]{1,0:T(8,128)(2,1)} %bitcast.33, bf16[80,1728]{1,0:T(8,128)(2,1)S(1)} %copy-done), kind=kOutput, calls=%fused_computation.13 | convolution fusion | flops 707788800 | bytes 9943040
  227.5 0.0 reduce-scatter.4.cloned.1.call-update
  227.5 50.8 %all-gather.14.cloned.1.call-done = bf16[20480,80]{1,0:T(8,128)(2,1)} async-done(((bf16[2560,80]{1,0:T(8,128)(2,1)}), bf16[20480,80]{1,0:T(8,128)(2,1)}) %all-gather.14.cloned.1.call-update) | async-done | bytes 3276816 | tf_op jit(solution)/shard_map/all_gather | solution.py:32
  278.3 0.0 copy-done.4
  278.3 3.5 %fusion.1 = f32[80,640]{1,0:T(8,128)} fusion(bf16[2560,640]{1,0:T(8,128)(2,1)} %bitcast.37, bf16[8,2560,80]{2,1,0:T(8,128)(2,1)} %bitcast.43, s32[]{:T(128)S(6)} %select_n.38, f32[80,640]{1,0:T(8,128)S(1)} %copy-done.4, f32[]{:T(128)S(6)} %div.14, f32[]{:T(128)} %bitcast.30), kind=kOutput, calls=%fused_computation.4 | convolution fusion | flops 262297600 | bytes 4342280 | tf_op jit(solution)/shard_map/dot_general | solution.py:43
  281.8 0.0 copy-start.2
  281.8 6.1 %fusion.3 = f32[80,1728]{1,0:T(8,128)} fusion(bf16[2560,1728]{1,0:T(8,128)(2,1)} %bitcast.34, bf16[8,2560,80]{2,1,0:T(8,128)(2,1)} %bitcast.44, s32[]{:T(128)S(6)} %select_n.38), kind=kOutput, calls=%fused_computation.6 | convolution fusion | flops 707788800 | bytes 10383364 | tf_op jit(solution)/shard_map/dot_general | solution.py:43
  287.9 0.0 all-reduce.5.cloned.1.call-done
  287.9 0.0 copy-done.2
  287.9 7.4 %fusion = f32[216,1728]{1,0:T(8,128)} fusion(bf16[2560,216]{1,0:T(8,128)(2,1)} %all-reduce.5.cloned.1.call-done, bf16[2560,1728]{1,0:T(8,128)(2,1)} %bitcast.35, f32[216,1728]{1,0:T(8,128)S(1)} %copy-done.2, f32[]{:T(128)S(6)} %div.14, f32[]{:T(128)} %bitcast.32), kind=kOutput, calls=%fused_computation.1 | convolution fusion | flops 1912149504 | bytes 12939272 | tf_op jit(solution)/shard_map/dot_general | solution.py:43
  295.3 27.7 %reduce-scatter.4.cloned.1.call-done = f32[320,80]{1,0:T(8,128)} async-done(((f32[2560,80]{1,0:T(8,128)}), f32[320,80]{1,0:T(8,128)}) %reduce-scatter.4.cloned.1.call-update) | async-done | bytes 102416
  323.0 1.6 copy.18
  (1 shorter events, 0.0 us)
Async XLA Ops:
  8.0 212.2 %copy-start = (bf16[80,1728]{1,0:T(8,128)(2,1)S(1)}, bf16[80,1728]{1,0:T(8,128)(2,1)}, u32[]{:S(2)}) copy-start(bf16[80,1728]{1,0:T(8,128)(2,1)} %param.7) | copy-start | bytes 829444
  8.0 27.8 %copy-start.3 = (bf16[40,1728]{1,0:T(8,128)(2,1)S(1)}, bf16[40,1728]{1,0:T(8,128)(2,1)}, u32[]{:S(2)}) copy-start(bf16[40,1728]{1,0:T(8,128)(2,1)} %param.8) | copy-start | bytes 414724
  8.0 68.9 %all-gather.10.cloned.1.call-start = ((), (), s32[]{:S(2)}) async-start(), calls=%async_computation.3 | async-start | bytes 1433600 | tf_op jit(solution)/shard_map/all_gather | solution.py:20
  16.9 88.8 %all-gather.8.cloned.1.call-start = ((), (), s32[]{:S(2)}) async-start(), calls=%async_computation.2 | async-start | bytes 3686400 | tf_op jit(solution)/shard_map/all_gather | solution.py:20
  37.3 38.4 %all-to-all-start = ((bf16[40,64,216]{2,0,1:T(8,128)(2,1)}), bf16[40,64,216]{2,0,1:T(8,128)(2,1)S(1)}, u32[]{:S(2)}, u32[]{:S(2)}) async-start(bf16[40,64,216]{2,0,1:T(8,128)(2,1)} %bitcast.11), calls=%async_computation | async-start | bytes 2621440 | tf_op jit(solution)/shard_map/all_to_all | solution.py:71
  47.2 116.2 %all-reduce.3.cloned.1.call-start = ((), (), s32[]{:S(2)}) async-start(), calls=%async_computation.5 | async-start | bytes 2621440 | tf_op jit(solution)/shard_map/psum | solution.py:38
  76.9 135.5 %all-gather.12.cloned.1.call-start = ((), (), s32[]{:S(2)}) async-start(), calls=%async_computation.4 | async-start | bytes 10321920 | tf_op jit(solution)/shard_map/all_gather | solution.py:20
  77.6 200.7 %all-gather.14.cloned.1.call-start = ((), (), s32[]{:S(2)}) async-start(), calls=%async_computation.7 | async-start | bytes 5898240 | tf_op jit(solution)/shard_map/all_gather | solution.py:32
  108.0 1.7 copy-start.1
  111.0 176.9 %all-reduce.5.cloned.1.call-start = ((), (), s32[]{:S(2)}) async-start(), calls=%async_computation.6 | async-start | bytes 2621440 | tf_op jit(solution)/shard_map/psum | solution.py:38
  163.5 159.5 %reduce-scatter.4.cloned.1.call-start = ((), (), s32[]{:S(2)}) async-start(), calls=%async_computation.8 | async-start | bytes 1474560
  220.2 58.1 %copy-start.4 = (f32[80,640]{1,0:T(8,128)S(1)}, f32[80,640]{1,0:T(8,128)}, u32[]{:S(2)}) copy-start(f32[80,640]{1,0:T(8,128)} %param.9) | copy-start | bytes 614404
  281.8 6.1 %copy-start.2 = (f32[216,1728]{1,0:T(8,128)S(1)}, f32[216,1728]{1,0:T(8,128)}, u32[]{:S(2)}) copy-start(f32[216,1728]{1,0:T(8,128)} %param.10) | copy-start | bytes 4478980
Sparse Core Ops, SparseCore 0:
  17.0 36.9 all-gather.9
  56.1 49.5 all-gather.7
  107.7 104.5 all-gather.11
  214.4 63.8 all-gather.13
  281.0 42.0 reduce-scatter.3
Sparse Core Ops, SparseCore 1:
  76.9 86.5 all-reduce.2
  166.2 34.1 all-reduce.4
where the time goes:
time: 332 us
  waiting for transfers between devices  236 us (71%)
  blocking collectives  27.6 us (8%)
  matrix products  24.3 us (7%)
  local copies, waits for them, and re-layouts  16.2 us (5%)
  between operations  16 us (5%)
  starting transfers between devices  10.3 us (3%)
    all_gather x3, waiting for transfers between devices, all_blocks(): parts = lax.all_gather(parts, axes[k], axis=0, tiled=True)  76.2 us
    psum x2, waiting for transfers between devices, broadcast_by_axis(): x = lax.psum(x, axis)  52.4 us
    all_gather x1, waiting for transfers between devices, picked(): lax.all_gather(x, axis)  50.8 us
    unnamed x8, waiting for transfers between devices  28.5 us
    all_to_all x1, waiting for transfers between devices, local(): lax.all_to_all(spread, DP, split_axis=1, concat_axis=0, tiled=True)  28.4 us
    all_gather x3, blocking collectives, all_blocks(): parts = lax.all_gather(parts, axes[k], axis=0, tiled=True)  27.6 us
    dot_general x3, matrix products, contract_rows(): lax.dot_general(left, right, (((0,), (0,)), ((), ())), preferred_element_...  17 us
    transpose x2, local copies, waits for them, and re-layouts, all_blocks(): parts.transpose(*turned, *range(len(sequence), parts.ndim))  10.2 us
  transfers between devices with their start and end apart: 8, of which 6 were waited for; matrix products, arithmetic and copies ran while one was open for 12% of the time, Pallas kernels for 0%

commit v1 on v0

v1 whole, which is shorter than its diff:
```python
import jax
import jax.numpy as jnp
from jax import lax
from jax.experimental import pallas as pl
from jax.experimental.pallas import tpu as pltpu
from jax.experimental.layout import Layout, with_layout_constraint
from jax.sharding import Mesh
from jax.sharding import PartitionSpec as P


AXES = ("dp_0", "dp_1", "dp_2", "tensor_0", "tensor_1")
DP = AXES[:3]
TENSOR = AXES[3:]
SIZES = (4, 2, 8, 4, 2)
X, ZL, Y, ZH, C = range(5)


def number(at):
    total = 0
    for place, size in zip(at, SIZES, strict=True):
        total = total * size + place % size
    return total


def pairs_of(move):
    out = []
    for i in range(512):
        at, rest = [], i
        for size in reversed(SIZES):
            at.append(rest % size)
            rest //= size
        at = at[::-1]
        out.append((i, number(move(list(at)))))
    return out


def towards(dim, turn):
    def move(at):
        step = 1 if (at[dim] + at[C]) % 2 == 0 else -1
        at[dim] += step if turn == 0 else -step
        return at

    return pairs_of(move)


def flipped(dim):
    def move(at):
        at[dim] = 1 - at[dim]
        return at

    return pairs_of(move)


def shifted(dim, by):
    def move(at):
        at[dim] += by
        return at

    return pairs_of(move)


Y_A, Y_B = towards(Y, 0), towards(Y, 1)
X_A, X_B = towards(X, 0), towards(X, 1)
H_A, H_B = towards(ZH, 0), towards(ZH, 1)
ZL_SWAP, C_SWAP = flipped(ZL), flipped(C)
TURN = pairs_of(lambda at: [at[ZH], at[C], at[Y], at[X], at[ZL]])


def rows_major(x):
    return with_layout_constraint(x, Layout(major_to_minor=tuple(range(x.ndim))))


def send(x, pairs):
    return rows_major(lax.ppermute(rows_major(x), AXES, pairs))


def contract_rows(left, right):
    return lax.dot_general(
        left, right, (((0,), (0,)), ((), ())), preferred_element_type=jnp.float32
    )


def contract_cols(left, right):
    return lax.dot_general(
        left, right, (((1,), (1,)), ((), ())), preferred_element_type=jnp.float32
    )


def copy_block(_, source, target):
    target[...] = source[...]


def picked_blocks(x, order):
    block = (1, *x.shape[1:])
    return pl.pallas_call(
        copy_block,
        grid_spec=pltpu.PrefetchScalarGridSpec(
            num_scalar_prefetch=1,
            grid=(x.shape[0],),
            in_specs=[pl.BlockSpec(block, lambda i, at: (at[i], 0, 0))],
            out_specs=pl.BlockSpec(block, lambda i, at: (i, 0, 0)),
        ),
        out_shape=jax.ShapeDtypeStruct(x.shape, x.dtype),
        name="picked_blocks",
    )(order, x)


def sign(n):
    return 1 - 2 * (n % 2)


def local(layer_input, up_weight, grad_output, factor_input, factor_grad, decay):
    tokens = layer_input.shape[0]
    feats, units = up_weight.shape[0], factor_grad.shape[0]
    wide_x, wide_g = layer_input.shape[1], grad_output.shape[1]
    token_total = tokens * 64
    keep = decay[0]
    blend = (1.0 - keep) / token_total
    x, zl, y, zh, c = (lax.axis_index(a) for a in AXES)
    own_core = c == zl
    dx, dy = sign(x + c), sign(y + c)

    p0 = jnp.concatenate([layer_input, grad_output], axis=1)
    q_own = send(grad_output, ZL_SWAP)

    def along_y(own):
        a1 = send(own, Y_A)
        a2 = send(jnp.concatenate([own, a1], 0), Y_B)
        a3 = send(a2, Y_A)
        a4 = send(a3, Y_B)
        return a1, a2, a3, a4

    n = tokens
    a1, a2, a3, a4 = along_y(p0)
    by_y = jnp.zeros((8, n, wide_x + wide_g), p0.dtype)
    for piece, k in (
        (p0, 0), (a1, 1), (a2[:n], -1), (a2[n:], -2),
        (a3[:n], 2), (a3[n:], 3), (a4[:n], -3), (a4[n:], -4),
    ):
        by_y = lax.dynamic_update_index_in_dim(by_y, piece, (y + dy * k) % 8, 0)
    rows = 8 * n
    by_y = by_y.reshape(rows, wide_x + wide_g)
    p1 = send(by_y, X_A)
    p2 = send(by_y, X_B)
    p3 = send(p1, X_B)
    p_wide = (by_y, p1, p2, p3)

    b1 = send(q_own, X_A)
    b2 = send(jnp.concatenate([q_own, b1], 0), X_B)
    by_x = jnp.zeros((4, n, wide_g), q_own.dtype)
    for piece, k in ((q_own, 0), (b1, 1), (b2[:n], -1), (b2[n:], -2)):
        by_x = lax.dynamic_update_index_in_dim(by_x, piece, (x + dx * k) % 4, 0)
    by_x = by_x.reshape(4 * n, wide_g)
    q_wide = (by_x, *along_y(by_x))

    part = jnp.concatenate(
        [
            lax.dynamic_slice_in_dim(by_y, y * feats, feats, 1),
            lax.dynamic_slice_in_dim(by_y, wide_x + y * units, units, 1),
        ],
        axis=1,
    )
    narrow = feats + units
    h0 = send(part, TURN)
    h1 = send(h0, H_A)
    h2 = send(jnp.concatenate([h0, h1], 0), H_B)
    mine = jnp.concatenate([h0, h1, h2], 0)
    theirs = send(mine, C_SWAP)
    n_own = jnp.where(own_core, mine, theirs)
    n_other = jnp.where(own_core, theirs, mine)
    n_cross = send(n_other[:, :feats], ZL_SWAP)

    def place(x_at, step):
        off = (x_at - zh) * step % 4
        return off ^ (off >> 1)

    order_k = jnp.array([0, 1, -1, -2], jnp.int32)
    order_p = place((x + dx * order_k) % 4, sign(zh + zl))
    l_own = picked_blocks(
        jnp.concatenate([n_own, n_cross], 1).reshape(4, rows, narrow + feats), order_p
    ).reshape(4 * rows, narrow + feats)
    order_y = (y + dy * jnp.array([0, 1, -1, -2, 2, 3, -3, -4], jnp.int32)) % 8
    x_at = jnp.arange(4, dtype=jnp.int32)
    order_q = place(x_at[None, :], sign(zh + 1 - zl)) * 8 + order_y[:, None]
    l_other = picked_blocks(n_other.reshape(32, n, narrow), order_q.reshape(32)).reshape(
        4 * rows, narrow
    )

    total = None
    fi_total = None
    gi_p, gi_q = [], []
    at = 0
    for piece in q_wide:
        got = contract_rows(l_other[at : at + piece.shape[0]], piece)
        total = got if total is None else total + got
        gi_q.append(contract_cols(piece, up_weight))
        at += piece.shape[0]
    at = 0
    for piece in p_wide:
        left = l_own[at : at + piece.shape[0]]
        right_x, right_g = piece[:, :wide_x], piece[:, wide_x:]
        total = total + contract_rows(left[:, :narrow], right_g)
        got = contract_rows(
            jnp.concatenate([left[:, :feats], left[:, narrow:]], 1), right_x
        )
        fi_total = got if fi_total is None else fi_total + got
        gi_p.append(contract_cols(right_g, up_weight))
        at += piece.shape[0]
    grad_weight = total[:feats]
    new_factor_grad = keep * factor_grad + blend * total[feats:]
    fi_got = send(fi_total[feats:], ZL_SWAP)
    new_factor_input = keep * factor_input + blend * (fi_total[:feats] + fi_got)

    gi_p = jnp.concatenate(gi_p, 0).reshape(4, rows, feats)
    back = (x_at - x) * dx % 4
    gi_p = picked_blocks(gi_p, back ^ (back >> 1)).reshape(4, rows, feats)
    gi_q = jnp.concatenate(gi_q, 0).reshape(32, n, feats)
    back_y = (jnp.arange(8, dtype=jnp.int32) - y) * dy % 8
    spot = jnp.where(
        back_y < 2, back_y, jnp.where(back_y < 4, back_y + 2, jnp.where(back_y < 6, 11 - back_y, 9 - back_y))
    )
    gi_q = picked_blocks(gi_q, (spot[None, :] * 4 + x_at[:, None]).reshape(32)).reshape(
        4, rows, feats
    )
    gi_keep = jnp.where(own_core, gi_p, gi_q)
    gi_send = jnp.where(own_core, gi_q, gi_p)
    half = gi_keep + send(gi_send, C_SWAP)
    out = lax.dynamic_index_in_dim(half, zh, 0, keepdims=False)
    for by in (1, 3, 2):
        piece = lax.dynamic_index_in_dim(half, (zh + by) % 4, 0, keepdims=False)
        out = out + send(piece, shifted(ZH, by))
    return (grad_weight, out.astype(jnp.bfloat16), new_factor_input, new_factor_grad)


def solution(mesh):
    finer = Mesh(mesh.devices.reshape(SIZES), AXES)

    return jax.shard_map(
        local,
        mesh=finer,
        in_specs=(P(DP, TENSOR), P(DP, TENSOR), P(DP, TENSOR), P(DP, TENSOR), P(DP, TENSOR), P()),
        out_specs=(P(DP, TENSOR), P(TENSOR, DP), P(DP, TENSOR), P(DP, TENSOR)),
        check_vma=False,
    )
```

time: 332 us -> 286 us (0.86)
  the two profiles are of different devices: /device:TPU:6 before, /device:TPU:1 now
where the time goes in v1:
time: 286 us; the launch traced here: 281 us
  starting transfers between devices  117 us (41%)
  waiting for transfers between devices  40.8 us (14%)
  matrix products  40.3 us (14%)
  Pallas kernels  39.3 us (14%)
  local copies, waits for them, and re-layouts  29 us (10%)
  other arithmetic  12 us (4%)
    ppermute x24, starting transfers between devices, send(): return rows_major(lax.ppermute(rows_major(x), AXES, pairs))  117 us
    ppermute x24, waiting for transfers between devices, send(): return rows_major(lax.ppermute(rows_major(x), AXES, pairs))  40.8 us
    pallas_call x4, Pallas kernels, picked_blocks(): pl.pallas_call(copy_block, grid_spec=pltpu.PrefetchScalarGridSpec(num_sca...  39.3 us
    dot_general x13, matrix products, contract_rows(): lax.dot_general(left, right, (((0,), (0,)), ((), ())), preferred_element_...  23.9 us
    dot_general x9, matrix products, contract_cols(): lax.dot_general(left, right, (((1,), (1,)), ((), ())), preferred_element_...  16.4 us
  transfers between devices with their start and end apart: 24, of which 8 were waited for; matrix products, arithmetic and copies ran while one was open for 28% of the time, Pallas kernels for 14%

profile of v1, /device:TPU:1, one launch (start us, length us, event | category | flops | bytes accessed | tf_op | source)
XLA Modules:
  0.0 281.2 jit_solution(12929572010256704168)
XLA Ops:
  0.6 5.0 %collective-permute-start.8 = (bf16[40,1728]{1,0:T(8,128)(2,1)}, bf16[40,1728]{1,0:T(8,128)(2,1)S(1)}, u32[]{:S(2)}, u32[]{:S(2)}) collective-permute-start(bf16[40,1728]{1,0:T(8,128)(2,1)} %param.10), channel_id=1, source_target_pairs={{0,64},{1,65},{2,66},{3,67},{4,68},{5,69},{6,70},{7,71},{8,72},{9,... | collective-permute-start | bytes 414728 | tf_op jit(solution)/shard_map/ppermute | solution.py:74
  7.3 5.1 %collective-permute-start = (bf16[40,2368]{1,0:T(8,128)(2,1)S(1)}, bf16[40,2368]{1,0:T(8,128)(2,1)S(1)}, u32[]{:S(2)}, u32[]{:S(2)}) collective-permute-start(bf16[40,2368]{1,0:T(8,128)(2,1)S(1)} %constant_dynamic-update-slice_fusion), channel_id=1, source_target_pairs={{0,8},{1,57},{2,10},{3,59},{4,12},{5,61},{6,14},{7,63},{8,0},{9,17... | collective-permute-start | bytes 568328 | tf_op jit(solution)/shard_map/ppermute | solution.py:74
  16.0 4.4 %collective-permute-start.9 = (bf16[40,1728]{1,0:T(8,128)(2,1)S(1)}, bf16[40,1728]{1,0:T(8,128)(2,1)S(1)}, u32[]{:S(2)}, u32[]{:S(2)}) collective-permute-start(bf16[40,1728]{1,0:T(8,128)(2,1)S(1)} %collective-permute-done.8), channel_id=1, source_target_pairs={{0,128},{1,385},{2,130},{3,387},{4,132},{5,389},{6,134},{7,391},{8... | collective-permute-start | bytes 414728 | tf_op jit(solution)/shard_map/ppermute | solution.py:74
  25.1 5.6 %collective-permute-done.10 = bf16[80,1728]{1,0:T(8,128)(2,1)S(1)} collective-permute-done((bf16[80,1728]{1,0:T(8,128)(2,1)S(1)}, bf16[80,1728]{1,0:T(8,128)(2,1)S(1)}, u32[]{:S(2)}, u32[]{:S(2)}) %collective-permute-start.10) | collective-permute-done | bytes 276512 | tf_op jit(solution)/shard_map/ppermute | solution.py:74
  30.8 3.5 %collective-permute-start.11 = (bf16[160,1728]{1,0:T(8,128)(2,1)S(1)}, bf16[160,1728]{1,0:T(8,128)(2,1)S(1)}, u32[]{:S(2)}, u32[]{:S(2)}) collective-permute-start(bf16[160,1728]{1,0:T(8,128)(2,1)S(1)} %bitcast.113), channel_id=1, source_target_pairs={{0,8},{1,57},{2,10},{3,59},{4,12},{5,61},{6,14},{7,63},{8,0},{9,17... | collective-permute-start | bytes 1658888 | tf_op jit(solution)/shard_map/ppermute | solution.py:74
  34.3 3.0 %collective-permute-start.2 = (bf16[80,2368]{1,0:T(8,128)(2,1)S(1)}, bf16[80,2368]{1,0:T(8,128)(2,1)S(1)}, u32[]{:S(2)}, u32[]{:S(2)}) collective-permute-start(bf16[80,2368]{1,0:T(8,128)(2,1)S(1)} %collective-permute-done.1), channel_id=1, source_target_pairs={{0,8},{1,57},{2,10},{3,59},{4,12},{5,61},{6,14},{7,63},{8,0},{9,17... | collective-permute-start | bytes 1136648 | tf_op jit(solution)/shard_map/ppermute | solution.py:74
  37.4 9.2 %collective-permute-done.2 = bf16[80,2368]{1,0:T(8,128)(2,1)S(1)} collective-permute-done((bf16[80,2368]{1,0:T(8,128)(2,1)S(1)}, bf16[80,2368]{1,0:T(8,128)(2,1)S(1)}, u32[]{:S(2)}, u32[]{:S(2)}) %collective-permute-start.2) | collective-permute-done | bytes 378912 | tf_op jit(solution)/shard_map/ppermute | solution.py:74
  46.6 2.2 collective-permute-start.3
  48.9 6.2 %collective-permute-done.3 = bf16[80,2368]{1,0:T(8,128)(2,1)S(1)} collective-permute-done((bf16[80,2368]{1,0:T(8,128)(2,1)S(1)}, bf16[80,2368]{1,0:T(8,128)(2,1)S(1)}, u32[]{:S(2)}, u32[]{:S(2)}) %collective-permute-start.3) | collective-permute-done | bytes 378912 | tf_op jit(solution)/shard_map/ppermute | solution.py:74
  55.5 9.0 %collective-permute-start.4 = (bf16[320,296]{1,0:T(8,128)(2,1)S(1)}, bf16[320,296]{1,0:T(8,128)(2,1)S(1)}, u32[]{:S(2)}, u32[]{:S(2)}) collective-permute-start(bf16[320,296]{1,0:T(8,128)(2,1)S(1)} %pad_maximum_fusion.5), channel_id=1, source_target_pairs={{0,0},{1,64},{2,128},{3,192},{4,256},{5,320},{6,384},{7,448},{8,8}... | collective-permute-start | bytes 568328 | tf_op jit(solution)/shard_map/ppermute | solution.py:74
  65.1 7.4 %collective-permute-done.4 = bf16[320,296]{1,0:T(8,128)(2,1)S(1)} collective-permute-done((bf16[320,296]{1,0:T(8,128)(2,1)S(1)}, bf16[320,296]{1,0:T(8,128)(2,1)S(1)}, u32[]{:S(2)}, u32[]{:S(2)}) %collective-permute-start.4) | collective-permute-done | bytes 189472 | tf_op jit(solution)/shard_map/ppermute | solution.py:74
  72.5 12.0 %collective-permute-start.5 = (bf16[320,296]{1,0:T(8,128)(2,1)S(1)}, bf16[320,296]{1,0:T(8,128)(2,1)S(1)}, u32[]{:S(2)}, u32[]{:S(2)}) collective-permute-start(bf16[320,296]{1,0:T(8,128)(2,1)S(1)} %collective-permute-done.4), channel_id=1, source_target_pairs={{0,2},{1,7},{2,0},{3,5},{4,6},{5,3},{6,4},{7,1},{8,10},{9,15},{10,... | collective-permute-start | bytes 568328 | tf_op jit(solution)/shard_map/ppermute | solution.py:74
  85.7 2.8 %collective-permute-start.12 = (bf16[320,1728]{1,0:T(8,128)(2,1)}, bf16[320,1728]{1,0:T(8,128)(2,1)}, u32[]{:S(2)}, u32[]{:S(2)}) collective-permute-start(bf16[320,1728]{1,0:T(8,128)(2,1)} %pad_maximum_fusion), channel_id=1, source_target_pairs={{0,56},{1,9},{2,58},{3,11},{4,60},{5,13},{6,62},{7,15},{8,16},{9,1... | collective-permute-start | bytes 3317768 | tf_op jit(solution)/shard_map/ppermute | solution.py:74
  92.6 14.6 %collective-permute-start.16 = (bf16[320,2368]{1,0:T(8,128)(2,1)S(1)}, bf16[320,2368]{1,0:T(8,128)(2,1)}, u32[]{:S(2)}, u32[]{:S(2)}) collective-permute-start(bf16[320,2368]{1,0:T(8,128)(2,1)S(1)} %bitcast.118), channel_id=1, source_target_pairs={{0,128},{1,385},{2,130},{3,387},{4,132},{5,389},{6,134},{7,391},{8... | collective-permute-start | bytes 4546568 | tf_op jit(solution)/shard_map/ppermute | solution.py:74
  109.6 2.2 copy.18
  111.8 14.0 %collective-permute-start.7 = (bf16[1280,296]{0,1:T(8,128)(2,1)}, bf16[1280,296]{0,1:T(8,128)(2,1)}, u32[]{:S(2)}, u32[]{:S(2)}) collective-permute-start(bf16[1280,296]{0,1:T(8,128)(2,1)} %copy.18), channel_id=1, source_target_pairs={{0,1},{1,0},{2,3},{3,2},{4,5},{5,4},{6,7},{7,6},{8,9},{9,8},{10,11... | collective-permute-start | bytes 2273288 | tf_op jit(solution)/shard_map/ppermute | solution.py:74
  129.8 3.5 %collective-permute-start.13 = (bf16[320,1728]{1,0:T(8,128)(2,1)}, bf16[320,1728]{1,0:T(8,128)(2,1)}, u32[]{:S(2)}, u32[]{:S(2)}) collective-permute-start(bf16[320,1728]{1,0:T(8,128)(2,1)} %collective-permute-done.12), channel_id=1, source_target_pairs={{0,8},{1,57},{2,10},{3,59},{4,12},{5,61},{6,14},{7,63},{8,0},{9,17... | collective-permute-start | bytes 3317768 | tf_op jit(solution)/shard_map/ppermute | solution.py:74
  133.3 2.4 fusion.77
  135.7 2.2 copy.19
  137.9 2.6 broadcast_select_fusion
  141.3 4.7 %collective-permute-start.15 = (bf16[1280,80]{1,0:T(8,128)(2,1)}, bf16[1280,80]{1,0:T(8,128)(2,1)}, u32[]{:S(2)}, u32[]{:S(2)}) collective-permute-start(bf16[1280,80]{1,0:T(8,128)(2,1)} %slice.213), channel_id=1, source_target_pairs={{0,64},{1,65},{2,66},{3,67},{4,68},{5,69},{6,70},{7,71},{8,72},{9,... | collective-permute-start | bytes 614408 | tf_op jit(solution)/shard_map/ppermute | solution.py:74
  146.0 15.9 %picked_blocks.4 = bf16[32,40,296]{2,1,0:T(8,128)(2,1)} custom-call(s32[32]{0:T(128)} %add.323._, bf16[32,40,296]{2,1,0:T(8,128)(2,1)} %bitcast.125), custom_call_target="tpu_custom_call" | custom-call | tf_op jit(solution)/shard_map/picked_blocks/pallas_call | solution.py:95
  161.9 3.5 %collective-permute-start.18 = (bf16[320,2368]{1,0:T(8,128)(2,1)}, bf16[320,2368]{1,0:T(8,128)(2,1)}, u32[]{:S(2)}, u32[]{:S(2)}) collective-permute-start(bf16[320,2368]{1,0:T(8,128)(2,1)} %collective-permute-done.16), channel_id=1, source_target_pairs={{0,384},{1,129},{2,386},{3,131},{4,388},{5,133},{6,390},{7,135},{8... | collective-permute-start | bytes 4546568 | tf_op jit(solution)/shard_map/ppermute | solution.py:74
  165.4 2.0 fusion.68
  167.5 2.4 fusion.12
  170.4 2.1 fusion.74
  174.4 2.5 fusion.8
  176.9 2.1 pad_maximum_fusion.1
  179.0 4.0 %picked_blocks.5 = bf16[4,320,376]{2,1,0:T(8,128)(2,1)} custom-call(s32[4]{0:T(128)} %shift-right-arithmetic_xor_fusion.1._, bf16[4,320,376]{2,1,0:T(8,128)(2,1)} %bitcast.127), custom_call_target="tpu_custom_call" | custom-call | tf_op jit(solution)/shard_map/picked_blocks/pallas_call | solution.py:95
  188.2 2.1 fusion.17
  190.3 3.5 %fusion.10 = f32[296,1728]{1,0:T(8,128)} fusion(bf16[320,2368]{1,0:T(8,128)(2,1)} %collective-permute-done.17, bf16[320,376]{1,0:T(8,128)(2,1)S(1)} %get-tuple-element.19), kind=kOutput, calls=%fused_computation.20 | convolution fusion | flops 327352320 | bytes 3433472 | tf_op jit(solution)/shard_map/dot_general | solution.py:78
  193.8 2.0 collective-permute-start.14
  195.8 2.4 fusion.78
  203.2 2.1 collective-permute-start.23
  205.3 2.4 fusion.5
  209.6 2.1 copy.20
  211.7 3.9 %picked_blocks.6 = f32[4,320,80]{2,1,0:T(8,128)} custom-call(s32[4]{0:T(128)} %get-tuple-element.38._, f32[4,320,80]{2,1,0:T(8,128)} %bitcast.128), custom_call_target="tpu_custom_call" | custom-call | tf_op jit(solution)/shard_map/picked_blocks/pallas_call | solution.py:95
  220.2 15.5 %picked_blocks.7 = f32[32,40,80]{2,1,0:T(8,128)} custom-call(s32[32]{0:T(128)} %add.382._, f32[32,40,80]{2,1,0:T(8,128)} %bitcast.129), custom_call_target="tpu_custom_call" | custom-call | tf_op jit(solution)/shard_map/picked_blocks/pallas_call | solution.py:95
  236.6 2.1 copy.22
  238.7 5.9 %collective-permute-start.19 = (f32[4,320,80]{1,2,0:T(8,128)}, f32[4,320,80]{1,2,0:T(8,128)}, u32[]{:S(2)}, u32[]{:S(2)}) collective-permute-start(f32[4,320,80]{1,2,0:T(8,128)} %copy.22), channel_id=1, source_target_pairs={{0,1},{1,0},{2,3},{3,2},{4,5},{5,4},{6,7},{7,6},{8,9},{9,8},{10,11... | collective-permute-start | bytes 1228808 | tf_op jit(solution)/shard_map/ppermute | solution.py:74
  244.7 2.9 %fusion.1 = f32[296,1728]{1,0:T(8,128)S(1)} fusion(f32[296,1728]{1,0:T(8,128)} %fusion.17, f32[296,1728]{1,0:T(8,128)S(1)} %convolution_add_fusion.3, bf16[320,296]{1,0:T(8,128)(2,1)S(1)} %bitcast.131, bf16[320,1728]{1,0:T(8,128)(2,1)} %copy-done.8), kind=kOutput, calls=%fused_computation.4 | convolution fusion | flops 328375296 | bytes 7433216 | tf_op jit(solution)/shard_map/dot_general | solution.py:78
  247.7 2.1 fusion
  249.8 2.1 convolution_add_fusion
  255.6 3.1 %collective-permute-start.20 = (f32[320,80]{1,0:T(8,128)S(1)}, f32[320,80]{1,0:T(8,128)S(1)}, u32[]{:S(2)}, u32[]{:S(2)}) collective-permute-start(f32[320,80]{1,0:T(8,128)S(1)} %get-tuple-element.25), channel_id=1, source_target_pairs={{0,2},{1,3},{2,4},{3,5},{4,6},{5,7},{6,0},{7,1},{8,10},{9,11},{10,... | collective-permute-start | bytes 307208 | tf_op jit(solution)/shard_map/ppermute | solution.py:74
  258.7 6.1 %collective-permute-start.22 = (f32[320,80]{1,0:T(8,128)S(1)}, f32[320,80]{1,0:T(8,128)S(1)}, u32[]{:S(2)}, u32[]{:S(2)}) collective-permute-start(f32[320,80]{1,0:T(8,128)S(1)} %get-tuple-element.26), channel_id=1, source_target_pairs={{0,4},{1,5},{2,6},{3,7},{4,0},{5,1},{6,2},{7,3},{8,12},{9,13},{10,... | collective-permute-start | bytes 307208 | tf_op jit(solution)/shard_map/ppermute | solution.py:74
  264.8 3.3 %collective-permute-start.21 = (f32[320,80]{1,0:T(8,128)S(1)}, f32[320,80]{1,0:T(8,128)S(1)}, u32[]{:S(2)}, u32[]{:S(2)}) collective-permute-start(f32[320,80]{1,0:T(8,128)S(1)} %get-tuple-element.27), channel_id=1, source_target_pairs={{0,6},{1,7},{2,0},{3,1},{4,2},{5,3},{6,4},{7,5},{8,14},{9,15},{10,... | collective-permute-start | bytes 307208 | tf_op jit(solution)/shard_map/ppermute | solution.py:74
  269.8 7.6 %collective-permute-done.22 = f32[320,80]{1,0:T(8,128)S(1)} collective-permute-done((f32[320,80]{1,0:T(8,128)S(1)}, f32[320,80]{1,0:T(8,128)S(1)}, u32[]{:S(2)}, u32[]{:S(2)}) %collective-permute-start.22) | collective-permute-done | bytes 102432 | tf_op jit(solution)/shard_map/ppermute | solution.py:74
  277.5 2.9 %collective-permute-done.21 = f32[320,80]{1,0:T(8,128)S(1)} collective-permute-done((f32[320,80]{1,0:T(8,128)S(1)}, f32[320,80]{1,0:T(8,128)S(1)}, u32[]{:S(2)}, u32[]{:S(2)}) %collective-permute-start.21) | collective-permute-done | bytes 102432 | tf_op jit(solution)/shard_map/ppermute | solution.py:74
  (131 shorter events, 48.4 us)
Async XLA Ops:
  0.6 91.1 %copy-start = (bf16[80,1728]{1,0:T(8,128)(2,1)S(1)}, bf16[80,1728]{1,0:T(8,128)(2,1)}, u32[]{:S(2)}) copy-start(bf16[80,1728]{1,0:T(8,128)(2,1)} %param.9) | copy-start | bytes 829444
  0.6 15.4 %collective-permute-start.8 = (bf16[40,1728]{1,0:T(8,128)(2,1)}, bf16[40,1728]{1,0:T(8,128)(2,1)S(1)}, u32[]{:S(2)}, u32[]{:S(2)}) collective-permute-start(bf16[40,1728]{1,0:T(8,128)(2,1)} %param.10), channel_id=1, source_target_pairs={{0,64},{1,65},{2,66},{3,67},{4,68},{5,69},{6,70},{7,71},{8,72},{9,... | collective-permute-start | bytes 414728 | tf_op jit(solution)/shard_map/ppermute | solution.py:74
  7.3 13.1 %collective-permute-start = (bf16[40,2368]{1,0:T(8,128)(2,1)S(1)}, bf16[40,2368]{1,0:T(8,128)(2,1)S(1)}, u32[]{:S(2)}, u32[]{:S(2)}) collective-permute-start(bf16[40,2368]{1,0:T(8,128)(2,1)S(1)} %constant_dynamic-update-slice_fusion), channel_id=1, source_target_pairs={{0,8},{1,57},{2,10},{3,59},{4,12},{5,61},{6,14},{7,63},{8,0},{9,17... | collective-permute-start | bytes 568328 | tf_op jit(solution)/shard_map/ppermute | solution.py:74
  16.0 7.0 %collective-permute-start.9 = (bf16[40,1728]{1,0:T(8,128)(2,1)S(1)}, bf16[40,1728]{1,0:T(8,128)(2,1)S(1)}, u32[]{:S(2)}, u32[]{:S(2)}) collective-permute-start(bf16[40,1728]{1,0:T(8,128)(2,1)S(1)} %collective-permute-done.8), channel_id=1, source_target_pairs={{0,128},{1,385},{2,130},{3,387},{4,132},{5,389},{6,134},{7,391},{8... | collective-permute-start | bytes 414728 | tf_op jit(solution)/shard_map/ppermute | solution.py:74
  20.5 13.8 %collective-permute-start.1 = (bf16[80,2368]{1,0:T(8,128)(2,1)S(1)}, bf16[80,2368]{1,0:T(8,128)(2,1)S(1)}, u32[]{:S(2)}, u32[]{:S(2)}) collective-permute-start(bf16[80,2368]{1,0:T(8,128)(2,1)S(1)} %pad_maximum_fusion.3), channel_id=1, source_target_pairs={{0,56},{1,9},{2,58},{3,11},{4,60},{5,13},{6,62},{7,15},{8,16},{9,1... | collective-permute-start | bytes 1136648 | tf_op jit(solution)/shard_map/ppermute | solution.py:74
  23.1 7.7 %collective-permute-start.10 = (bf16[80,1728]{1,0:T(8,128)(2,1)S(1)}, bf16[80,1728]{1,0:T(8,128)(2,1)S(1)}, u32[]{:S(2)}, u32[]{:S(2)}) collective-permute-start(bf16[80,1728]{1,0:T(8,128)(2,1)S(1)} %pad_maximum_fusion.4), channel_id=1, source_target_pairs={{0,384},{1,129},{2,386},{3,131},{4,388},{5,133},{6,390},{7,135},{8... | collective-permute-start | bytes 829448 | tf_op jit(solution)/shard_map/ppermute | solution.py:74
  30.8 53.7 %collective-permute-start.11 = (bf16[160,1728]{1,0:T(8,128)(2,1)S(1)}, bf16[160,1728]{1,0:T(8,128)(2,1)S(1)}, u32[]{:S(2)}, u32[]{:S(2)}) collective-permute-start(bf16[160,1728]{1,0:T(8,128)(2,1)S(1)} %bitcast.113), channel_id=1, source_target_pairs={{0,8},{1,57},{2,10},{3,59},{4,12},{5,61},{6,14},{7,63},{8,0},{9,17... | collective-permute-start | bytes 1658888 | tf_op jit(solution)/shard_map/ppermute | solution.py:74
  34.3 12.3 %collective-permute-start.2 = (bf16[80,2368]{1,0:T(8,128)(2,1)S(1)}, bf16[80,2368]{1,0:T(8,128)(2,1)S(1)}, u32[]{:S(2)}, u32[]{:S(2)}) collective-permute-start(bf16[80,2368]{1,0:T(8,128)(2,1)S(1)} %collective-permute-done.1), channel_id=1, source_target_pairs={{0,8},{1,57},{2,10},{3,59},{4,12},{5,61},{6,14},{7,63},{8,0},{9,17... | collective-permute-start | bytes 1136648 | tf_op jit(solution)/shard_map/ppermute | solution.py:74
  37.4 27.2 %copy-start.21 = (s32[4]{0:T(128)S(1)}, s32[4]{0:T(128)}, u32[]{:S(2)}) copy-start(s32[4]{0:T(128)} %constant.238.clone) | copy-start | bytes 52
  46.6 8.5 %collective-permute-start.3 = (bf16[80,2368]{1,0:T(8,128)(2,1)S(1)}, bf16[80,2368]{1,0:T(8,128)(2,1)S(1)}, u32[]{:S(2)}, u32[]{:S(2)}) collective-permute-start(bf16[80,2368]{1,0:T(8,128)(2,1)S(1)} %collective-permute-done.2), channel_id=1, source_target_pairs={{0,56},{1,9},{2,58},{3,11},{4,60},{5,13},{6,62},{7,15},{8,16},{9,1... | collective-permute-start | bytes 1136648 | tf_op jit(solution)/shard_map/ppermute | solution.py:74
  55.5 17.0 %collective-permute-start.4 = (bf16[320,296]{1,0:T(8,128)(2,1)S(1)}, bf16[320,296]{1,0:T(8,128)(2,1)S(1)}, u32[]{:S(2)}, u32[]{:S(2)}) collective-permute-start(bf16[320,296]{1,0:T(8,128)(2,1)S(1)} %pad_maximum_fusion.5), channel_id=1, source_target_pairs={{0,0},{1,64},{2,128},{3,192},{4,256},{5,320},{6,384},{7,448},{8,8}... | collective-permute-start | bytes 568328 | tf_op jit(solution)/shard_map/ppermute | solution.py:74
  72.5 17.2 %collective-permute-start.5 = (bf16[320,296]{1,0:T(8,128)(2,1)S(1)}, bf16[320,296]{1,0:T(8,128)(2,1)S(1)}, u32[]{:S(2)}, u32[]{:S(2)}) collective-permute-start(bf16[320,296]{1,0:T(8,128)(2,1)S(1)} %collective-permute-done.4), channel_id=1, source_target_pairs={{0,2},{1,7},{2,0},{3,5},{4,6},{5,3},{6,4},{7,1},{8,10},{9,15},{10,... | collective-permute-start | bytes 568328 | tf_op jit(solution)/shard_map/ppermute | solution.py:74
  84.5 41.2 %copy-start.6 = (bf16[160,1728]{1,0:T(8,128)(2,1)}, bf16[160,1728]{1,0:T(8,128)(2,1)S(1)}, u32[]{:S(2)}) copy-start(bf16[160,1728]{1,0:T(8,128)(2,1)S(1)} %collective-permute-done.11) | copy-start | bytes 1658884
  85.7 44.1 %collective-permute-start.12 = (bf16[320,1728]{1,0:T(8,128)(2,1)}, bf16[320,1728]{1,0:T(8,128)(2,1)}, u32[]{:S(2)}, u32[]{:S(2)}) collective-permute-start(bf16[320,1728]{1,0:T(8,128)(2,1)} %pad_maximum_fusion), channel_id=1, source_target_pairs={{0,56},{1,9},{2,58},{3,11},{4,60},{5,13},{6,62},{7,15},{8,16},{9,1... | collective-permute-start | bytes 3317768 | tf_op jit(solution)/shard_map/ppermute | solution.py:74
  89.8 19.0 %collective-permute-start.6 = (bf16[640,296]{1,0:T(8,128)(2,1)S(1)}, bf16[640,296]{1,0:T(8,128)(2,1)S(1)}, u32[]{:S(2)}, u32[]{:S(2)}) collective-permute-start(bf16[640,296]{1,0:T(8,128)(2,1)S(1)} %pad_maximum_fusion.2), channel_id=1, source_target_pairs={{0,6},{1,3},{2,4},{3,1},{4,2},{5,7},{6,0},{7,5},{8,14},{9,11},{10,... | collective-permute-start | bytes 1136648 | tf_op jit(solution)/shard_map/ppermute | solution.py:74
  92.6 69.3 %collective-permute-start.16 = (bf16[320,2368]{1,0:T(8,128)(2,1)S(1)}, bf16[320,2368]{1,0:T(8,128)(2,1)}, u32[]{:S(2)}, u32[]{:S(2)}) collective-permute-start(bf16[320,2368]{1,0:T(8,128)(2,1)S(1)} %bitcast.118), channel_id=1, source_target_pairs={{0,128},{1,385},{2,130},{3,387},{4,132},{5,389},{6,134},{7,391},{8... | collective-permute-start | bytes 4546568 | tf_op jit(solution)/shard_map/ppermute | solution.py:74
  111.8 23.9 %collective-permute-start.7 = (bf16[1280,296]{0,1:T(8,128)(2,1)}, bf16[1280,296]{0,1:T(8,128)(2,1)}, u32[]{:S(2)}, u32[]{:S(2)}) collective-permute-start(bf16[1280,296]{0,1:T(8,128)(2,1)} %copy.18), channel_id=1, source_target_pairs={{0,1},{1,0},{2,3},{3,2},{4,5},{5,4},{6,7},{7,6},{8,9},{9,8},{10,11... | collective-permute-start | bytes 2273288 | tf_op jit(solution)/shard_map/ppermute | solution.py:74
  126.7 47.7 %collective-permute-start.17 = (bf16[320,2368]{1,0:T(8,128)(2,1)S(1)}, bf16[320,2368]{1,0:T(8,128)(2,1)}, u32[]{:S(2)}, u32[]{:S(2)}) collective-permute-start(bf16[320,2368]{1,0:T(8,128)(2,1)S(1)} %bitcast.119), channel_id=1, source_target_pairs={{0,384},{1,129},{2,386},{3,131},{4,388},{5,133},{6,390},{7,135},{8... | collective-permute-start | bytes 4546568 | tf_op jit(solution)/shard_map/ppermute | solution.py:74
  129.8 64.0 %collective-permute-start.13 = (bf16[320,1728]{1,0:T(8,128)(2,1)}, bf16[320,1728]{1,0:T(8,128)(2,1)}, u32[]{:S(2)}, u32[]{:S(2)}) collective-permute-start(bf16[320,1728]{1,0:T(8,128)(2,1)} %collective-permute-done.12), channel_id=1, source_target_pairs={{0,8},{1,57},{2,10},{3,59},{4,12},{5,61},{6,14},{7,63},{8,0},{9,17... | collective-permute-start | bytes 3317768 | tf_op jit(solution)/shard_map/ppermute | solution.py:74
  140.5 5.5 %copy-start.5 = (bf16[1280,296]{1,0:T(8,128)(2,1)}, bf16[1280,296]{1,0:T(8,128)(2,1)S(1)}, u32[]{:S(2)}) copy-start(bf16[1280,296]{1,0:T(8,128)(2,1)S(1)} %get-tuple-element.17) | copy-start | bytes 2273284
  141.3 35.6 %collective-permute-start.15 = (bf16[1280,80]{1,0:T(8,128)(2,1)}, bf16[1280,80]{1,0:T(8,128)(2,1)}, u32[]{:S(2)}, u32[]{:S(2)}) collective-permute-start(bf16[1280,80]{1,0:T(8,128)(2,1)} %slice.213), channel_id=1, source_target_pairs={{0,64},{1,65},{2,66},{3,67},{4,68},{5,69},{6,70},{7,71},{8,72},{9,... | collective-permute-start | bytes 614408 | tf_op jit(solution)/shard_map/ppermute | solution.py:74
  161.9 8.0 %copy-start.7 = (bf16[160,1728]{1,0:T(8,128)(2,1)S(1)}, bf16[160,1728]{1,0:T(8,128)(2,1)}, u32[]{:S(2)}) copy-start(bf16[160,1728]{1,0:T(8,128)(2,1)} %copy-done.6) | copy-start | bytes 1658884
  161.9 8.0 %slice-start = ((bf16[32,40,296]{2,1,0:T(8,128)(2,1)}), bf16[4,40,296]{2,1,0:T(8,128)(2,1)S(1)}, s32[]{:S(2)}) async-start(bf16[32,40,296]{2,1,0:T(8,128)(2,1)} %picked_blocks.4), calls=%async_computation | async-start | bytes 245760 | tf_op jit(solution)/shard_map/slice | solution.py:194
  161.9 38.3 %collective-permute-start.18 = (bf16[320,2368]{1,0:T(8,128)(2,1)}, bf16[320,2368]{1,0:T(8,128)(2,1)}, u32[]{:S(2)}, u32[]{:S(2)}) collective-permute-start(bf16[320,2368]{1,0:T(8,128)(2,1)} %collective-permute-done.16), channel_id=1, source_target_pairs={{0,384},{1,129},{2,386},{3,131},{4,388},{5,133},{6,390},{7,135},{8... | collective-permute-start | bytes 4546568 | tf_op jit(solution)/shard_map/ppermute | solution.py:74
  170.4 2.1 copy-start.9
  174.4 2.5 copy-start.10
  184.5 2.2 copy-start.11
  184.5 2.2 copy-start.13
  190.3 8.0 %copy-start.2 = (f32[296,1728]{1,0:T(8,128)S(1)}, f32[296,1728]{1,0:T(8,128)}, u32[]{:S(2)}) copy-start(f32[296,1728]{1,0:T(8,128)} %fusion.3) | copy-start | bytes 6137860
  193.8 4.5 %copy-start.19 = (bf16[8,40,296]{2,1,0:T(8,128)(2,1)S(1)}, bf16[8,40,296]{2,1,0:T(8,128)(2,1)}, u32[]{:S(2)}) copy-start(bf16[8,40,296]{2,1,0:T(8,128)(2,1)} %get-tuple-element.23) | copy-start | bytes 568324
  193.8 21.8 %collective-permute-start.14 = (bf16[320,1728]{1,0:T(8,128)(2,1)}, bf16[320,1728]{1,0:T(8,128)(2,1)S(1)}, u32[]{:S(2)}, u32[]{:S(2)}) collective-permute-start(bf16[320,1728]{1,0:T(8,128)(2,1)} %collective-permute-done.13), channel_id=1, source_target_pairs={{0,56},{1,9},{2,58},{3,11},{4,60},{5,13},{6,62},{7,15},{8,16},{9,1... | collective-permute-start | bytes 3317768 | tf_op jit(solution)/shard_map/ppermute | solution.py:74
  201.7 0.8 copy-start.15
  203.2 65.0 %collective-permute-start.23 = (f32[80,640]{1,0:T(8,128)}, f32[80,640]{1,0:T(8,128)}, u32[]{:S(2)}, u32[]{:S(2)}) collective-permute-start(f32[80,640]{1,0:T(8,128)} %slice.240), channel_id=1, source_target_pairs={{0,64},{1,65},{2,66},{3,67},{4,68},{5,69},{6,70},{7,71},{8,72},{9,... | collective-permute-start | bytes 614408 | tf_op jit(solution)/shard_map/ppermute | solution.py:74
  215.6 1.0 copy-start.8
  217.8 17.9 %copy-start.3 = (f32[4,320,80]{2,1,0:T(8,128)S(1)}, f32[4,320,80]{2,1,0:T(8,128)}, u32[]{:S(2)}) copy-start(f32[4,320,80]{2,1,0:T(8,128)} %picked_blocks.6) | copy-start | bytes 1228804
  235.7 9.0 %copy-start.18 = (bf16[8,40,296]{2,1,0:T(8,128)(2,1)S(1)}, bf16[8,40,296]{2,1,0:T(8,128)(2,1)}, u32[]{:S(2)}) copy-start(bf16[8,40,296]{2,1,0:T(8,128)(2,1)} %get-tuple-element.22) | copy-start | bytes 568324
  238.7 15.3 %collective-permute-start.19 = (f32[4,320,80]{1,2,0:T(8,128)}, f32[4,320,80]{1,2,0:T(8,128)}, u32[]{:S(2)}, u32[]{:S(2)}) collective-permute-start(f32[4,320,80]{1,2,0:T(8,128)} %copy.22), channel_id=1, source_target_pairs={{0,1},{1,0},{2,3},{3,2},{4,5},{5,4},{6,7},{7,6},{8,9},{9,8},{10,11... | collective-permute-start | bytes 1228808 | tf_op jit(solution)/shard_map/ppermute | solution.py:74
  244.7 2.9 %copy-start.1 = (f32[296,1728]{1,0:T(8,128)S(1)}, f32[296,1728]{1,0:T(8,128)}, u32[]{:S(2)}) copy-start(f32[296,1728]{1,0:T(8,128)} %fusion.10) | copy-start | bytes 6137860
  244.7 2.9 %copy-start.14 = (bf16[320,376]{1,0:T(8,128)(2,1)S(1)}, bf16[320,376]{1,0:T(8,128)(2,1)}, u32[]{:S(2)}) copy-start(bf16[320,376]{1,0:T(8,128)(2,1)} %copy-done.13) | copy-start | bytes 721924
  247.7 2.1 copy-start.12
  249.8 3.0 %copy-start.17 = (f32[216,1728]{1,0:T(8,128)S(1)}, f32[216,1728]{1,0:T(8,128)}, u32[]{:S(2)}) copy-start(f32[216,1728]{1,0:T(8,128)} %param.12) | copy-start | bytes 4478980
  254.1 1.3 copy-start.4
  255.4 12.7 %copy-start.16 = (f32[160,640]{1,0:T(8,128)S(1)}, f32[160,640]{1,0:T(8,128)}, u32[]{:S(2)}) copy-start(f32[160,640]{1,0:T(8,128)} %copy-done.15) | copy-start | bytes 1228804
  255.4 12.7 %copy-start.20 = (f32[80,640]{1,0:T(8,128)S(1)}, f32[80,640]{1,0:T(8,128)}, u32[]{:S(2)}) copy-start(f32[80,640]{1,0:T(8,128)} %param.11) | copy-start | bytes 614404
  255.6 14.2 %collective-permute-start.20 = (f32[320,80]{1,0:T(8,128)S(1)}, f32[320,80]{1,0:T(8,128)S(1)}, u32[]{:S(2)}, u32[]{:S(2)}) collective-permute-start(f32[320,80]{1,0:T(8,128)S(1)} %get-tuple-element.25), channel_id=1, source_target_pairs={{0,2},{1,3},{2,4},{3,5},{4,6},{5,7},{6,0},{7,1},{8,10},{9,11},{10,... | collective-permute-start | bytes 307208 | tf_op jit(solution)/shard_map/ppermute | solution.py:74
  258.7 18.7 %collective-permute-start.22 = (f32[320,80]{1,0:T(8,128)S(1)}, f32[320,80]{1,0:T(8,128)S(1)}, u32[]{:S(2)}, u32[]{:S(2)}) collective-permute-start(f32[320,80]{1,0:T(8,128)S(1)} %get-tuple-element.26), channel_id=1, source_target_pairs={{0,4},{1,5},{2,6},{3,7},{4,0},{5,1},{6,2},{7,3},{8,12},{9,13},{10,... | collective-permute-start | bytes 307208 | tf_op jit(solution)/shard_map/ppermute | solution.py:74
  264.8 15.6 %collective-permute-start.21 = (f32[320,80]{1,0:T(8,128)S(1)}, f32[320,80]{1,0:T(8,128)S(1)}, u32[]{:S(2)}, u32[]{:S(2)}) collective-permute-start(f32[320,80]{1,0:T(8,128)S(1)} %get-tuple-element.27), channel_id=1, source_target_pairs={{0,6},{1,7},{2,0},{3,1},{4,2},{5,3},{6,4},{7,5},{8,14},{9,15},{10,... | collective-permute-start | bytes 307208 | tf_op jit(solution)/shard_map/ppermute | solution.py:74

commit v2 on v1

v2 whole, which is shorter than its diff:
```python
import jax
import jax.numpy as jnp
from jax import lax
from jax.experimental.layout import Layout, with_layout_constraint
from jax.sharding import Mesh
from jax.sharding import PartitionSpec as P


AXES = ("dp_0", "dp_1", "dp_2", "tensor_0", "tensor_1")
DP = AXES[:3]
TENSOR = AXES[3:]
SIZES = (4, 2, 8, 4, 2)
X, ZL, Y, ZH, C = range(5)


def number(at):
    total = 0
    for place, size in zip(at, SIZES, strict=True):
        total = total * size + place % size
    return total


def pairs_of(move):
    out = []
    for i in range(512):
        at, rest = [], i
        for size in reversed(SIZES):
            at.append(rest % size)
            rest //= size
        at = at[::-1]
        out.append((i, number(move(list(at)))))
    return out


def towards(dim, turn):
    def move(at):
        step = 1 if (at[dim] + at[C]) % 2 == 0 else -1
        at[dim] += step if turn == 0 else -step
        return at

    return pairs_of(move)


def flipped(dim):
    def move(at):
        at[dim] = 1 - at[dim]
        return at

    return pairs_of(move)


Y_A, Y_B = towards(Y, 0), towards(Y, 1)
X_A, X_B = towards(X, 0), towards(X, 1)
H_A, H_B = towards(ZH, 0), towards(ZH, 1)
ZL_SWAP, C_SWAP = flipped(ZL), flipped(C)
TURN = pairs_of(lambda at: [at[ZH], at[C], at[Y], at[X], at[ZL]])


def rows_major(x):
    return with_layout_constraint(x, Layout(major_to_minor=tuple(range(x.ndim))))


def send(x, pairs):
    return rows_major(lax.ppermute(rows_major(x), AXES, pairs))


def contract_rows(left, right):
    return rows_major(
        lax.dot_general(
            left, right, (((0,), (0,)), ((), ())), preferred_element_type=jnp.float32
        )
    )


def contract_cols(left, right):
    return lax.dot_general(
        left, right, (((1,), (1,)), ((), ())), preferred_element_type=jnp.float32
    )


def placed(blocks, spots, count):
    whole = jnp.zeros((count, *blocks[0].shape), blocks[0].dtype)
    for block, spot in zip(blocks, spots, strict=True):
        whole = lax.dynamic_update_index_in_dim(whole, block, spot, 0)
    return whole


def row_of(x, at):
    return lax.dynamic_index_in_dim(x, at, 0, keepdims=False)


def sign(n):
    return 1 - 2 * (n % 2)


def local(layer_input, up_weight, grad_output, factor_input, factor_grad, decay):
    n = layer_input.shape[0]
    feats, units = up_weight.shape[0], factor_grad.shape[0]
    wide_x, wide_g = layer_input.shape[1], grad_output.shape[1]
    keep = decay[0]
    blend = (1.0 - keep) / (n * 64)
    x, zl, y, zh, c = (lax.axis_index(a) for a in AXES)
    own_core = c == zl
    dx, dy, dh = sign(x + c), sign(y + c), sign(zh + c)
    rows = 8 * n

    def along_y(own):
        a1 = send(own, Y_A)
        a2 = send(jnp.concatenate([own, a1], 0), Y_B)
        a3 = send(a2, Y_A)
        a4 = send(a3, Y_B)
        m = own.shape[0]
        blocks = (own, a1, a2[:m], a2[m:], a3[:m], a3[m:], a4[:m], a4[m:])
        return blocks, [(y + dy * k) % 8 for k in (0, 1, -1, -2, 2, 3, -3, -4)]

    def along_x(own):
        b1 = send(own, X_A)
        b2 = send(jnp.concatenate([own, b1], 0), X_B)
        m = own.shape[0]
        return placed((own, b1, b2[:m], b2[m:]), x_spots, 4)

    x_spots = [(x + dx * k) % 4 for k in (0, 1, -1, -2)]

    spare = jnp.zeros((n, -(wide_x + wide_g) % 128), grad_output.dtype)
    p0 = jnp.concatenate([layer_input, grad_output, spare], axis=1)
    by_y = placed(*along_y(p0), 8).reshape(rows, -1)
    p1 = send(by_y, X_A)
    p2 = send(by_y, X_B)
    p3 = send(p1, X_B)
    p_wide = (by_y, p1, p2, p3)

    by_x = along_x(send(grad_output, ZL_SWAP)).reshape(4 * n, wide_g)
    q_wide = placed(*along_y(by_x), 8).reshape(4 * rows, wide_g)

    w_pair = jnp.concatenate([up_weight, send(up_weight, ZL_SWAP)], 0)
    w_all = along_x(w_pair)
    w_own, w_other = (w.reshape(4 * feats, wide_g) for w in (w_all[:, :feats], w_all[:, feats:]))
    w_keep = jnp.where(own_core, w_own, w_other)
    w_send = jnp.where(own_core, w_other, w_own)

    part = jnp.concatenate(
        [
            lax.dynamic_slice_in_dim(by_y, y * feats, 128, 1),
            lax.dynamic_slice_in_dim(by_y, wide_x + y * units, 256, 1),
        ],
        axis=1,
    )
    h0 = send(part, TURN)
    h1 = send(h0, H_A)
    h2 = send(jnp.concatenate([h0, h1], 0), H_B)
    mine = placed(
        (h0, h1, h2[:rows], h2[rows:]), [(zh + dh * k) % 4 for k in (0, 1, -1, -2)], 4
    ).reshape(4 * rows, -1)
    theirs = send(mine, C_SWAP)
    n_own = jnp.where(own_core, mine, theirs)
    n_other = jnp.where(own_core, theirs, mine)
    n_cross = send(n_other[:, :128], ZL_SWAP)
    n_fi = jnp.concatenate([n_own[:, :128], n_cross], 1).reshape(4, rows, 256)
    n_own = n_own.reshape(4, rows, -1)

    mine_g = by_y[:, wide_x : wide_x + wide_g]
    half = contract_cols(w_keep, mine_g) + send(contract_cols(w_send, mine_g), C_SWAP)
    half = half.reshape(4, feats, rows)
    far = jnp.concatenate([row_of(half, (zh - dh) % 4), row_of(half, (zh - 2 * dh) % 4)], 0)
    far = send(far, H_B)
    near = row_of(half, (zh + dh) % 4) + far[feats:]
    grad_input = row_of(half, zh) + far[:feats] + send(near, H_A)
    grad_input = send(grad_input.astype(jnp.bfloat16), TURN).T

    n_other = n_other.reshape(4, 8, n, -1).transpose(1, 0, 2, 3).reshape(4 * rows, -1)
    total, fi_total = contract_rows(n_other, q_wide), 0.0
    for piece, spot in zip(p_wide, x_spots):
        total = total + contract_rows(row_of(n_own, spot), piece[:, wide_x : wide_x + wide_g])
        fi_total = fi_total + contract_rows(row_of(n_fi, spot), piece[:, :wide_x])
    grad_weight = total[:feats]
    new_factor_grad = keep * factor_grad + blend * total[128 : 128 + units]
    fi_got = send(fi_total[128 : 128 + feats], ZL_SWAP)
    new_factor_input = keep * factor_input + blend * (fi_total[:feats] + fi_got)
    return (grad_weight, grad_input, new_factor_input, new_factor_grad)


def solution(mesh):
    finer = Mesh(mesh.devices.reshape(SIZES), AXES)

    return jax.shard_map(
        local,
        mesh=finer,
        in_specs=(P(DP, TENSOR), P(DP, TENSOR), P(DP, TENSOR), P(DP, TENSOR), P(DP, TENSOR), P()),
        out_specs=(P(DP, TENSOR), P(TENSOR, DP), P(DP, TENSOR), P(DP, TENSOR)),
        check_vma=False,
    )
```

time: 286 us -> 181 us (0.63)
  the two profiles are of different devices: /device:TPU:1 before, /device:TPU:6 now
where the time goes in v2:
time: 181 us; the launch traced here: 179 us
  starting transfers between devices  101 us (56%)
  waiting for transfers between devices  58.5 us (32%)
  matrix products  8.86 us (5%)
  local copies, waits for them, and re-layouts  4.68 us (3%)
  other arithmetic  2.99 us (2%)
  between operations  2.52 us (1%)
    ppermute x27, starting transfers between devices, send(): return rows_major(lax.ppermute(rows_major(x), AXES, pairs))  101 us
    ppermute x27, waiting for transfers between devices, send(): return rows_major(lax.ppermute(rows_major(x), AXES, pairs))  58.5 us
    dot_general x9, matrix products, contract_rows(): lax.dot_general(left, right, (((0,), (0,)), ((), ())), preferred_element_...  7.32 us
  transfers between devices with their start and end apart: 27, of which 12 were waited for; matrix products, arithmetic and copies ran while one was open for 8% of the time, Pallas kernels for 0%

profile of v2, /device:TPU:6, one launch (start us, length us, event | category | flops | bytes accessed | tf_op | source)
XLA Modules:
  0.0 178.9 jit_solution(13617247384472505252)
XLA Ops:
  0.6 4.4 %collective-permute-start.8 = (bf16[40,1728]{1,0:T(8,128)(2,1)}, bf16[40,1728]{1,0:T(8,128)(2,1)S(1)}, u32[]{:S(2)}, u32[]{:S(2)}) collective-permute-start(bf16[40,1728]{1,0:T(8,128)(2,1)} %param.8), channel_id=1, source_target_pairs={{0,64},{1,65},{2,66},{3,67},{4,68},{5,69},{6,70},{7,71},{8,72},{9,... | collective-permute-start | bytes 414728 | tf_op jit(solution)/shard_map/ppermute | solution.py:64
  5.1 1.0 concatenate.31
  6.1 3.5 %collective-permute-start = (bf16[40,2432]{1,0:T(8,128)(2,1)S(1)}, bf16[40,2432]{1,0:T(8,128)(2,1)S(1)}, u32[]{:S(2)}, u32[]{:S(2)}) collective-permute-start(bf16[40,2432]{1,0:T(8,128)(2,1)S(1)} %concatenate.31), channel_id=1, source_target_pairs={{0,8},{1,57},{2,10},{3,59},{4,12},{5,61},{6,14},{7,63},{8,0},{9,17... | collective-permute-start | bytes 583688 | tf_op jit(solution)/shard_map/ppermute | solution.py:64
  9.6 1.9 %collective-permute-start.18 = (bf16[80,1728]{1,0:T(8,128)(2,1)}, bf16[80,1728]{1,0:T(8,128)(2,1)S(1)}, u32[]{:S(2)}, u32[]{:S(2)}) collective-permute-start(bf16[80,1728]{1,0:T(8,128)(2,1)} %param.7), channel_id=1, source_target_pairs={{0,64},{1,65},{2,66},{3,67},{4,68},{5,69},{6,70},{7,71},{8,72},{9,... | collective-permute-start | bytes 829448 | tf_op jit(solution)/shard_map/ppermute | solution.py:64
  12.8 2.7 %collective-permute-start.9 = (bf16[40,1728]{1,0:T(8,128)(2,1)S(1)}, bf16[40,1728]{1,0:T(8,128)(2,1)S(1)}, u32[]{:S(2)}, u32[]{:S(2)}) collective-permute-start(bf16[40,1728]{1,0:T(8,128)(2,1)S(1)} %collective-permute-done.8), channel_id=1, source_target_pairs={{0,128},{1,385},{2,130},{3,387},{4,132},{5,389},{6,134},{7,391},{8... | collective-permute-start | bytes 414728 | tf_op jit(solution)/shard_map/ppermute | solution.py:64
  15.7 5.1 %collective-permute-start.1 = (bf16[80,2432]{1,0:T(8,128)(2,1)S(1)}, bf16[80,2432]{1,0:T(8,128)(2,1)S(1)}, u32[]{:S(2)}, u32[]{:S(2)}) collective-permute-start(bf16[80,2432]{1,0:T(8,128)(2,1)S(1)} %pad_maximum_fusion.4), channel_id=1, source_target_pairs={{0,56},{1,9},{2,58},{3,11},{4,60},{5,13},{6,62},{7,15},{8,16},{9,1... | collective-permute-start | bytes 1167368 | tf_op jit(solution)/shard_map/ppermute | solution.py:64
  21.2 2.8 %collective-permute-start.19 = (bf16[160,1728]{1,0:T(8,128)(2,1)S(1)}, bf16[160,1728]{1,0:T(8,128)(2,1)S(1)}, u32[]{:S(2)}, u32[]{:S(2)}) collective-permute-start(bf16[160,1728]{1,0:T(8,128)(2,1)S(1)} %constant_dynamic-update-slice_fusion), channel_id=1, source_target_pairs={{0,128},{1,385},{2,130},{3,387},{4,132},{5,389},{6,134},{7,391},{8... | collective-permute-start | bytes 1658888 | tf_op jit(solution)/shard_map/ppermute | solution.py:64
  24.3 3.0 %collective-permute-start.10 = (bf16[80,1728]{1,0:T(8,128)(2,1)S(1)}, bf16[80,1728]{1,0:T(8,128)(2,1)S(1)}, u32[]{:S(2)}, u32[]{:S(2)}) collective-permute-start(bf16[80,1728]{1,0:T(8,128)(2,1)S(1)} %pad_maximum_fusion.5), channel_id=1, source_target_pairs={{0,384},{1,129},{2,386},{3,131},{4,388},{5,133},{6,390},{7,135},{8... | collective-permute-start | bytes 829448 | tf_op jit(solution)/shard_map/ppermute | solution.py:64
  27.3 8.9 %collective-permute-done.10 = bf16[80,1728]{1,0:T(8,128)(2,1)S(1)} collective-permute-done((bf16[80,1728]{1,0:T(8,128)(2,1)S(1)}, bf16[80,1728]{1,0:T(8,128)(2,1)S(1)}, u32[]{:S(2)}, u32[]{:S(2)}) %collective-permute-start.10) | collective-permute-done | bytes 276512 | tf_op jit(solution)/shard_map/ppermute | solution.py:64
  36.3 1.9 %collective-permute-start.11 = (bf16[160,1728]{1,0:T(8,128)(2,1)S(1)}, bf16[160,1728]{1,0:T(8,128)(2,1)S(1)}, u32[]{:S(2)}, u32[]{:S(2)}) collective-permute-start(bf16[160,1728]{1,0:T(8,128)(2,1)S(1)} %bitcast.164), channel_id=1, source_target_pairs={{0,8},{1,57},{2,10},{3,59},{4,12},{5,61},{6,14},{7,63},{8,0},{9,17... | collective-permute-start | bytes 1658888 | tf_op jit(solution)/shard_map/ppermute | solution.py:64
  38.6 3.9 %collective-permute-start.2 = (bf16[80,2432]{1,0:T(8,128)(2,1)S(1)}, bf16[80,2432]{1,0:T(8,128)(2,1)S(1)}, u32[]{:S(2)}, u32[]{:S(2)}) collective-permute-start(bf16[80,2432]{1,0:T(8,128)(2,1)S(1)} %collective-permute-done.1), channel_id=1, source_target_pairs={{0,8},{1,57},{2,10},{3,59},{4,12},{5,61},{6,14},{7,63},{8,0},{9,17... | collective-permute-start | bytes 1167368 | tf_op jit(solution)/shard_map/ppermute | solution.py:64
  42.7 2.2 %collective-permute-start.20 = (bf16[320,1728]{1,0:T(8,128)(2,1)S(1)}, bf16[320,1728]{1,0:T(8,128)(2,1)S(1)}, u32[]{:S(2)}, u32[]{:S(2)}) collective-permute-start(bf16[320,1728]{1,0:T(8,128)(2,1)S(1)} %pad_maximum_fusion.1), channel_id=1, source_target_pairs={{0,384},{1,129},{2,386},{3,131},{4,388},{5,133},{6,390},{7,135},{8... | collective-permute-start | bytes 3317768 | tf_op jit(solution)/shard_map/ppermute | solution.py:64
  45.0 7.1 %collective-permute-done.2 = bf16[80,2432]{1,0:T(8,128)(2,1)S(1)} collective-permute-done((bf16[80,2432]{1,0:T(8,128)(2,1)S(1)}, bf16[80,2432]{1,0:T(8,128)(2,1)S(1)}, u32[]{:S(2)}, u32[]{:S(2)}) %collective-permute-start.2) | collective-permute-done | bytes 389152 | tf_op jit(solution)/shard_map/ppermute | solution.py:64
  52.1 1.9 %collective-permute-start.3 = (bf16[80,2432]{1,0:T(8,128)(2,1)S(1)}, bf16[80,2432]{1,0:T(8,128)(2,1)S(1)}, u32[]{:S(2)}, u32[]{:S(2)}) collective-permute-start(bf16[80,2432]{1,0:T(8,128)(2,1)S(1)} %collective-permute-done.2), channel_id=1, source_target_pairs={{0,56},{1,9},{2,58},{3,11},{4,60},{5,13},{6,62},{7,15},{8,16},{9,1... | collective-permute-start | bytes 1167368 | tf_op jit(solution)/shard_map/ppermute | solution.py:64
  54.1 8.8 %collective-permute-done.3 = bf16[80,2432]{1,0:T(8,128)(2,1)S(1)} collective-permute-done((bf16[80,2432]{1,0:T(8,128)(2,1)S(1)}, bf16[80,2432]{1,0:T(8,128)(2,1)S(1)}, u32[]{:S(2)}, u32[]{:S(2)}) %collective-permute-start.3) | collective-permute-done | bytes 389152 | tf_op jit(solution)/shard_map/ppermute | solution.py:64
  63.3 10.0 %collective-permute-start.4 = (bf16[320,384]{1,0:T(8,128)(2,1)S(1)}, bf16[320,384]{1,0:T(8,128)(2,1)S(1)}, u32[]{:S(2)}, u32[]{:S(2)}) collective-permute-start(bf16[320,384]{1,0:T(8,128)(2,1)S(1)} %pad_maximum_fusion.6), channel_id=1, source_target_pairs={{0,0},{1,64},{2,128},{3,192},{4,256},{5,320},{6,384},{7,448},{8,8}... | collective-permute-start | bytes 737288 | tf_op jit(solution)/shard_map/ppermute | solution.py:64
  73.3 3.7 %collective-permute-start.12 = (bf16[320,1728]{1,0:T(8,128)(2,1)S(1)}, bf16[320,1728]{1,0:T(8,128)(2,1)S(1)}, u32[]{:S(2)}, u32[]{:S(2)}) collective-permute-start(bf16[320,1728]{1,0:T(8,128)(2,1)S(1)} %pad_maximum_fusion), channel_id=1, source_target_pairs={{0,56},{1,9},{2,58},{3,11},{4,60},{5,13},{6,62},{7,15},{8,16},{9,1... | collective-permute-start | bytes 3317768 | tf_op jit(solution)/shard_map/ppermute | solution.py:64
  77.0 10.9 %collective-permute-done.4 = bf16[320,384]{1,0:T(8,128)(2,1)S(1)} collective-permute-done((bf16[320,384]{1,0:T(8,128)(2,1)S(1)}, bf16[320,384]{1,0:T(8,128)(2,1)S(1)}, u32[]{:S(2)}, u32[]{:S(2)}) %collective-permute-start.4) | collective-permute-done | bytes 245792 | tf_op jit(solution)/shard_map/ppermute | solution.py:64
  87.9 1.9 %collective-permute-start.5 = (bf16[320,384]{1,0:T(8,128)(2,1)S(1)}, bf16[320,384]{1,0:T(8,128)(2,1)S(1)}, u32[]{:S(2)}, u32[]{:S(2)}) collective-permute-start(bf16[320,384]{1,0:T(8,128)(2,1)S(1)} %collective-permute-done.4), channel_id=1, source_target_pairs={{0,2},{1,7},{2,0},{3,5},{4,6},{5,3},{6,4},{7,1},{8,10},{9,15},{10,... | collective-permute-start | bytes 737288 | tf_op jit(solution)/shard_map/ppermute | solution.py:64
  89.9 2.6 %collective-permute-start.15 = (bf16[320,2432]{1,0:T(8,128)(2,1)S(1)}, bf16[320,2432]{1,0:T(8,128)(2,1)S(1)}, u32[]{:S(2)}, u32[]{:S(2)}) collective-permute-start(bf16[320,2432]{1,0:T(8,128)(2,1)S(1)} %bitcast.152), channel_id=1, source_target_pairs={{0,128},{1,385},{2,130},{3,387},{4,132},{5,389},{6,134},{7,391},{8... | collective-permute-start | bytes 4669448 | tf_op jit(solution)/shard_map/ppermute | solution.py:64
  92.5 1.9 %collective-permute-start.16 = (bf16[320,2432]{1,0:T(8,128)(2,1)S(1)}, bf16[320,2432]{1,0:T(8,128)(2,1)S(1)}, u32[]{:S(2)}, u32[]{:S(2)}) collective-permute-start(bf16[320,2432]{1,0:T(8,128)(2,1)S(1)} %bitcast.153), channel_id=1, source_target_pairs={{0,384},{1,129},{2,386},{3,131},{4,388},{5,133},{6,390},{7,135},{8... | collective-permute-start | bytes 4669448 | tf_op jit(solution)/shard_map/ppermute | solution.py:64
  94.5 2.7 %collective-permute-done.5 = bf16[320,384]{1,0:T(8,128)(2,1)S(1)} collective-permute-done((bf16[320,384]{1,0:T(8,128)(2,1)S(1)}, bf16[320,384]{1,0:T(8,128)(2,1)S(1)}, u32[]{:S(2)}, u32[]{:S(2)}) %collective-permute-start.5) | collective-permute-done | bytes 245792 | tf_op jit(solution)/shard_map/ppermute | solution.py:64
  97.3 5.8 %collective-permute-start.6 = (bf16[640,384]{1,0:T(8,128)(2,1)S(1)}, bf16[640,384]{1,0:T(8,128)(2,1)S(1)}, u32[]{:S(2)}, u32[]{:S(2)}) collective-permute-start(bf16[640,384]{1,0:T(8,128)(2,1)S(1)} %pad_maximum_fusion.3), channel_id=1, source_target_pairs={{0,6},{1,3},{2,4},{3,1},{4,2},{5,7},{6,0},{7,5},{8,14},{9,11},{10,... | collective-permute-start | bytes 1474568 | tf_op jit(solution)/shard_map/ppermute | solution.py:64
  103.5 0.8 fusion.6
  104.2 1.9 %collective-permute-start.21 = (f32[320,320]{1,0:T(8,128)S(1)}, f32[320,320]{1,0:T(8,128)S(1)}, u32[]{:S(2)}, u32[]{:S(2)}) collective-permute-start(f32[320,320]{1,0:T(8,128)S(1)} %fusion.6), channel_id=1, source_target_pairs={{0,1},{1,0},{2,3},{3,2},{4,5},{5,4},{6,7},{7,6},{8,9},{9,8},{10,11... | collective-permute-start | bytes 1228808 | tf_op jit(solution)/shard_map/ppermute | solution.py:64
  106.2 2.2 %collective-permute-start.13 = (bf16[320,1728]{1,0:T(8,128)(2,1)S(1)}, bf16[320,1728]{1,0:T(8,128)(2,1)S(1)}, u32[]{:S(2)}, u32[]{:S(2)}) collective-permute-start(bf16[320,1728]{1,0:T(8,128)(2,1)S(1)} %collective-permute-done.12), channel_id=1, source_target_pairs={{0,8},{1,57},{2,10},{3,59},{4,12},{5,61},{6,14},{7,63},{8,0},{9,17... | collective-permute-start | bytes 3317768 | tf_op jit(solution)/shard_map/ppermute | solution.py:64
  108.4 0.8 convolution_add_fusion.6
  109.3 1.9 %collective-permute-start.22 = (f32[160,320]{1,0:T(8,128)S(1)}, f32[160,320]{1,0:T(8,128)S(1)}, u32[]{:S(2)}, u32[]{:S(2)}) collective-permute-start(f32[160,320]{1,0:T(8,128)S(1)} %pad_maximum_fusion.7), channel_id=1, source_target_pairs={{0,6},{1,3},{2,4},{3,1},{4,2},{5,7},{6,0},{7,5},{8,14},{9,11},{10,... | collective-permute-start | bytes 614408 | tf_op jit(solution)/shard_map/ppermute | solution.py:64
  111.2 2.1 %collective-permute-done.6 = bf16[640,384]{1,0:T(8,128)(2,1)S(1)} collective-permute-done((bf16[640,384]{1,0:T(8,128)(2,1)S(1)}, bf16[640,384]{1,0:T(8,128)(2,1)S(1)}, u32[]{:S(2)}, u32[]{:S(2)}) %collective-permute-start.6) | collective-permute-done | bytes 491552 | tf_op jit(solution)/shard_map/ppermute | solution.py:64
  113.3 6.8 %collective-permute-done.22 = f32[160,320]{1,0:T(8,128)S(1)} collective-permute-done((f32[160,320]{1,0:T(8,128)S(1)}, f32[160,320]{1,0:T(8,128)S(1)}, u32[]{:S(2)}, u32[]{:S(2)}) %collective-permute-start.22) | collective-permute-done | bytes 204832 | tf_op jit(solution)/shard_map/ppermute | solution.py:64
  120.1 7.0 %collective-permute-start.23 = (f32[80,320]{1,0:T(8,128)S(1)}, f32[80,320]{1,0:T(8,128)S(1)}, u32[]{:S(2)}, u32[]{:S(2)}) collective-permute-start(f32[80,320]{1,0:T(8,128)S(1)} %slice_add_fusion.1), channel_id=1, source_target_pairs={{0,2},{1,7},{2,0},{3,5},{4,6},{5,3},{6,4},{7,1},{8,10},{9,15},{10,... | collective-permute-start | bytes 307208 | tf_op jit(solution)/shard_map/ppermute | solution.py:64
  127.2 1.9 %collective-permute-start.7 = (bf16[1280,384]{1,0:T(8,128)(2,1)S(1)}, bf16[1280,384]{1,0:T(8,128)(2,1)S(1)}, u32[]{:S(2)}, u32[]{:S(2)}) collective-permute-start(bf16[1280,384]{1,0:T(8,128)(2,1)S(1)} %bitcast.168), channel_id=1, source_target_pairs={{0,1},{1,0},{2,3},{3,2},{4,5},{5,4},{6,7},{7,6},{8,9},{9,8},{10,11... | collective-permute-start | bytes 2949128 | tf_op jit(solution)/shard_map/ppermute | solution.py:64
  129.1 2.2 %collective-permute-done.23 = f32[80,320]{1,0:T(8,128)S(1)} collective-permute-done((f32[80,320]{1,0:T(8,128)S(1)}, f32[80,320]{1,0:T(8,128)S(1)}, u32[]{:S(2)}, u32[]{:S(2)}) %collective-permute-start.23) | collective-permute-done | bytes 102432 | tf_op jit(solution)/shard_map/ppermute | solution.py:64
  131.3 7.9 %collective-permute-start.24 = (bf16[80,320]{1,0:T(8,128)(2,1)S(1)}, bf16[80,320]{1,0:T(8,128)(2,1)S(1)}, u32[]{:S(2)}, u32[]{:S(2)}) collective-permute-start(bf16[80,320]{1,0:T(8,128)(2,1)S(1)} %fusion.53), channel_id=1, source_target_pairs={{0,0},{1,64},{2,128},{3,192},{4,256},{5,320},{6,384},{7,448},{8,8}... | collective-permute-start | bytes 153608 | tf_op jit(solution)/shard_map/ppermute | solution.py:64
  139.3 2.4 %collective-permute-done.24 = bf16[80,320]{1,0:T(8,128)(2,1)S(1)} collective-permute-done((bf16[80,320]{1,0:T(8,128)(2,1)S(1)}, bf16[80,320]{1,0:T(8,128)(2,1)S(1)}, u32[]{:S(2)}, u32[]{:S(2)}) %collective-permute-start.24) | collective-permute-done | bytes 51232 | tf_op jit(solution)/shard_map/ppermute | solution.py:64
  141.6 1.9 %collective-permute-start.17 = (bf16[320,2432]{1,0:T(8,128)(2,1)S(1)}, bf16[320,2432]{1,0:T(8,128)(2,1)S(1)}, u32[]{:S(2)}, u32[]{:S(2)}) collective-permute-start(bf16[320,2432]{1,0:T(8,128)(2,1)S(1)} %collective-permute-done.15), channel_id=1, source_target_pairs={{0,384},{1,129},{2,386},{3,131},{4,388},{5,133},{6,390},{7,135},{8... | collective-permute-start | bytes 4669448 | tf_op jit(solution)/shard_map/ppermute | solution.py:64
  143.6 4.3 %collective-permute-start.14 = (bf16[320,1728]{1,0:T(8,128)(2,1)S(1)}, bf16[320,1728]{1,0:T(8,128)(2,1)S(1)}, u32[]{:S(2)}, u32[]{:S(2)}) collective-permute-start(bf16[320,1728]{1,0:T(8,128)(2,1)S(1)} %collective-permute-done.13), channel_id=1, source_target_pairs={{0,56},{1,9},{2,58},{3,11},{4,60},{5,13},{6,62},{7,15},{8,16},{9,1... | collective-permute-start | bytes 3317768 | tf_op jit(solution)/shard_map/ppermute | solution.py:64
  148.3 5.8 %collective-permute-start.25 = (bf16[1280,128]{1,0:T(8,128)(2,1)S(1)}, bf16[1280,128]{1,0:T(8,128)(2,1)S(1)}, u32[]{:S(2)}, u32[]{:S(2)}) collective-permute-start(bf16[1280,128]{1,0:T(8,128)(2,1)S(1)} %slice.173), channel_id=1, source_target_pairs={{0,64},{1,65},{2,66},{3,67},{4,68},{5,69},{6,70},{7,71},{8,72},{9,... | collective-permute-start | bytes 983048 | tf_op jit(solution)/shard_map/ppermute | solution.py:64
  154.1 0.9 fusion.9
  155.1 0.9 fusion.3
  156.1 5.6 %collective-permute-done.25 = bf16[1280,128]{1,0:T(8,128)(2,1)S(1)} collective-permute-done((bf16[1280,128]{1,0:T(8,128)(2,1)S(1)}, bf16[1280,128]{1,0:T(8,128)(2,1)S(1)}, u32[]{:S(2)}, u32[]{:S(2)}) %collective-permute-start.25) | collective-permute-done | bytes 327712 | tf_op jit(solution)/shard_map/ppermute | solution.py:64
  163.0 2.1 %convolution_add_fusion.2 = f32[384,1728]{1,0:T(8,128)S(1)} fusion(f32[384,1728]{1,0:T(8,128)S(1)} %fusion.9, bf16[1280,384]{1,0:T(8,128)(2,1)S(1)} %bitcast.158, bf16[1280,1728]{1,0:T(8,128)(2,1)S(1)} %bitcast.149), kind=kOutput, calls=%fused_computation.3 | convolution fusion | flops 1699356672 | bytes 10715136 | tf_op jit(solution)/shard_map/dot_general | solution.py:69
  165.1 1.0 fusion
  166.5 7.0 %collective-permute-start.26 = (f32[80,640]{1,0:T(8,128)S(1)}, f32[80,640]{1,0:T(8,128)S(1)}, u32[]{:S(2)}, u32[]{:S(2)}) collective-permute-start(f32[80,640]{1,0:T(8,128)S(1)} %slice.179), channel_id=1, source_target_pairs={{0,64},{1,65},{2,66},{3,67},{4,68},{5,69},{6,70},{7,71},{8,72},{9,... | collective-permute-start | bytes 614408 | tf_op jit(solution)/shard_map/ppermute | solution.py:64
  173.6 0.9 convolution_add_fusion
  174.5 1.4 fusion.1
  175.9 0.8 slice.165
  176.7 0.8 collective-permute-done.26
  (83 shorter events, 6.3 us)
Async XLA Ops:
  0.6 12.1 %copy-start.1 = (bf16[80,1728]{1,0:T(8,128)(2,1)S(1)}, bf16[80,1728]{1,0:T(8,128)(2,1)}, u32[]{:S(2)}) copy-start(bf16[80,1728]{1,0:T(8,128)(2,1)} %param.7) | copy-start | bytes 829444
  0.6 12.2 %collective-permute-start.8 = (bf16[40,1728]{1,0:T(8,128)(2,1)}, bf16[40,1728]{1,0:T(8,128)(2,1)S(1)}, u32[]{:S(2)}, u32[]{:S(2)}) collective-permute-start(bf16[40,1728]{1,0:T(8,128)(2,1)} %param.8), channel_id=1, source_target_pairs={{0,64},{1,65},{2,66},{3,67},{4,68},{5,69},{6,70},{7,71},{8,72},{9,... | collective-permute-start | bytes 414728 | tf_op jit(solution)/shard_map/ppermute | solution.py:64
  6.1 9.5 %collective-permute-start = (bf16[40,2432]{1,0:T(8,128)(2,1)S(1)}, bf16[40,2432]{1,0:T(8,128)(2,1)S(1)}, u32[]{:S(2)}, u32[]{:S(2)}) collective-permute-start(bf16[40,2432]{1,0:T(8,128)(2,1)S(1)} %concatenate.31), channel_id=1, source_target_pairs={{0,8},{1,57},{2,10},{3,59},{4,12},{5,61},{6,14},{7,63},{8,0},{9,17... | collective-permute-start | bytes 583688 | tf_op jit(solution)/shard_map/ppermute | solution.py:64
  9.6 11.6 %collective-permute-start.18 = (bf16[80,1728]{1,0:T(8,128)(2,1)}, bf16[80,1728]{1,0:T(8,128)(2,1)S(1)}, u32[]{:S(2)}, u32[]{:S(2)}) collective-permute-start(bf16[80,1728]{1,0:T(8,128)(2,1)} %param.7), channel_id=1, source_target_pairs={{0,64},{1,65},{2,66},{3,67},{4,68},{5,69},{6,70},{7,71},{8,72},{9,... | collective-permute-start | bytes 829448 | tf_op jit(solution)/shard_map/ppermute | solution.py:64
  12.8 11.4 %collective-permute-start.9 = (bf16[40,1728]{1,0:T(8,128)(2,1)S(1)}, bf16[40,1728]{1,0:T(8,128)(2,1)S(1)}, u32[]{:S(2)}, u32[]{:S(2)}) collective-permute-start(bf16[40,1728]{1,0:T(8,128)(2,1)S(1)} %collective-permute-done.8), channel_id=1, source_target_pairs={{0,128},{1,385},{2,130},{3,387},{4,132},{5,389},{6,134},{7,391},{8... | collective-permute-start | bytes 414728 | tf_op jit(solution)/shard_map/ppermute | solution.py:64
  15.7 22.9 %collective-permute-start.1 = (bf16[80,2432]{1,0:T(8,128)(2,1)S(1)}, bf16[80,2432]{1,0:T(8,128)(2,1)S(1)}, u32[]{:S(2)}, u32[]{:S(2)}) collective-permute-start(bf16[80,2432]{1,0:T(8,128)(2,1)S(1)} %pad_maximum_fusion.4), channel_id=1, source_target_pairs={{0,56},{1,9},{2,58},{3,11},{4,60},{5,13},{6,62},{7,15},{8,16},{9,1... | collective-permute-start | bytes 1167368 | tf_op jit(solution)/shard_map/ppermute | solution.py:64
  21.2 21.4 %collective-permute-start.19 = (bf16[160,1728]{1,0:T(8,128)(2,1)S(1)}, bf16[160,1728]{1,0:T(8,128)(2,1)S(1)}, u32[]{:S(2)}, u32[]{:S(2)}) collective-permute-start(bf16[160,1728]{1,0:T(8,128)(2,1)S(1)} %constant_dynamic-update-slice_fusion), channel_id=1, source_target_pairs={{0,128},{1,385},{2,130},{3,387},{4,132},{5,389},{6,134},{7,391},{8... | collective-permute-start | bytes 1658888 | tf_op jit(solution)/shard_map/ppermute | solution.py:64
  24.3 12.0 %collective-permute-start.10 = (bf16[80,1728]{1,0:T(8,128)(2,1)S(1)}, bf16[80,1728]{1,0:T(8,128)(2,1)S(1)}, u32[]{:S(2)}, u32[]{:S(2)}) collective-permute-start(bf16[80,1728]{1,0:T(8,128)(2,1)S(1)} %pad_maximum_fusion.5), channel_id=1, source_target_pairs={{0,384},{1,129},{2,386},{3,131},{4,388},{5,133},{6,390},{7,135},{8... | collective-permute-start | bytes 829448 | tf_op jit(solution)/shard_map/ppermute | solution.py:64
  36.3 36.9 %collective-permute-start.11 = (bf16[160,1728]{1,0:T(8,128)(2,1)S(1)}, bf16[160,1728]{1,0:T(8,128)(2,1)S(1)}, u32[]{:S(2)}, u32[]{:S(2)}) collective-permute-start(bf16[160,1728]{1,0:T(8,128)(2,1)S(1)} %bitcast.164), channel_id=1, source_target_pairs={{0,8},{1,57},{2,10},{3,59},{4,12},{5,61},{6,14},{7,63},{8,0},{9,17... | collective-permute-start | bytes 1658888 | tf_op jit(solution)/shard_map/ppermute | solution.py:64
  38.6 13.5 %collective-permute-start.2 = (bf16[80,2432]{1,0:T(8,128)(2,1)S(1)}, bf16[80,2432]{1,0:T(8,128)(2,1)S(1)}, u32[]{:S(2)}, u32[]{:S(2)}) collective-permute-start(bf16[80,2432]{1,0:T(8,128)(2,1)S(1)} %collective-permute-done.1), channel_id=1, source_target_pairs={{0,8},{1,57},{2,10},{3,59},{4,12},{5,61},{6,14},{7,63},{8,0},{9,17... | collective-permute-start | bytes 1167368 | tf_op jit(solution)/shard_map/ppermute | solution.py:64
  42.7 60.5 %collective-permute-start.20 = (bf16[320,1728]{1,0:T(8,128)(2,1)S(1)}, bf16[320,1728]{1,0:T(8,128)(2,1)S(1)}, u32[]{:S(2)}, u32[]{:S(2)}) collective-permute-start(bf16[320,1728]{1,0:T(8,128)(2,1)S(1)} %pad_maximum_fusion.1), channel_id=1, source_target_pairs={{0,384},{1,129},{2,386},{3,131},{4,388},{5,133},{6,390},{7,135},{8... | collective-permute-start | bytes 3317768 | tf_op jit(solution)/shard_map/ppermute | solution.py:64
  52.1 10.8 %collective-permute-start.3 = (bf16[80,2432]{1,0:T(8,128)(2,1)S(1)}, bf16[80,2432]{1,0:T(8,128)(2,1)S(1)}, u32[]{:S(2)}, u32[]{:S(2)}) collective-permute-start(bf16[80,2432]{1,0:T(8,128)(2,1)S(1)} %collective-permute-done.2), channel_id=1, source_target_pairs={{0,56},{1,9},{2,58},{3,11},{4,60},{5,13},{6,62},{7,15},{8,16},{9,1... | collective-permute-start | bytes 1167368 | tf_op jit(solution)/shard_map/ppermute | solution.py:64
  63.3 24.7 %collective-permute-start.4 = (bf16[320,384]{1,0:T(8,128)(2,1)S(1)}, bf16[320,384]{1,0:T(8,128)(2,1)S(1)}, u32[]{:S(2)}, u32[]{:S(2)}) collective-permute-start(bf16[320,384]{1,0:T(8,128)(2,1)S(1)} %pad_maximum_fusion.6), channel_id=1, source_target_pairs={{0,0},{1,64},{2,128},{3,192},{4,256},{5,320},{6,384},{7,448},{8,8}... | collective-permute-start | bytes 737288 | tf_op jit(solution)/shard_map/ppermute | solution.py:64
  73.3 32.8 %collective-permute-start.12 = (bf16[320,1728]{1,0:T(8,128)(2,1)S(1)}, bf16[320,1728]{1,0:T(8,128)(2,1)S(1)}, u32[]{:S(2)}, u32[]{:S(2)}) collective-permute-start(bf16[320,1728]{1,0:T(8,128)(2,1)S(1)} %pad_maximum_fusion), channel_id=1, source_target_pairs={{0,56},{1,9},{2,58},{3,11},{4,60},{5,13},{6,62},{7,15},{8,16},{9,1... | collective-permute-start | bytes 3317768 | tf_op jit(solution)/shard_map/ppermute | solution.py:64
  87.9 9.3 %collective-permute-start.5 = (bf16[320,384]{1,0:T(8,128)(2,1)S(1)}, bf16[320,384]{1,0:T(8,128)(2,1)S(1)}, u32[]{:S(2)}, u32[]{:S(2)}) collective-permute-start(bf16[320,384]{1,0:T(8,128)(2,1)S(1)} %collective-permute-done.4), channel_id=1, source_target_pairs={{0,2},{1,7},{2,0},{3,5},{4,6},{5,3},{6,4},{7,1},{8,10},{9,15},{10,... | collective-permute-start | bytes 737288 | tf_op jit(solution)/shard_map/ppermute | solution.py:64
  89.9 51.7 %collective-permute-start.15 = (bf16[320,2432]{1,0:T(8,128)(2,1)S(1)}, bf16[320,2432]{1,0:T(8,128)(2,1)S(1)}, u32[]{:S(2)}, u32[]{:S(2)}) collective-permute-start(bf16[320,2432]{1,0:T(8,128)(2,1)S(1)} %bitcast.152), channel_id=1, source_target_pairs={{0,128},{1,385},{2,130},{3,387},{4,132},{5,389},{6,134},{7,391},{8... | collective-permute-start | bytes 4669448 | tf_op jit(solution)/shard_map/ppermute | solution.py:64
  92.5 62.6 %collective-permute-start.16 = (bf16[320,2432]{1,0:T(8,128)(2,1)S(1)}, bf16[320,2432]{1,0:T(8,128)(2,1)S(1)}, u32[]{:S(2)}, u32[]{:S(2)}) collective-permute-start(bf16[320,2432]{1,0:T(8,128)(2,1)S(1)} %bitcast.153), channel_id=1, source_target_pairs={{0,384},{1,129},{2,386},{3,131},{4,388},{5,133},{6,390},{7,135},{8... | collective-permute-start | bytes 4669448 | tf_op jit(solution)/shard_map/ppermute | solution.py:64
  97.3 16.0 %collective-permute-start.6 = (bf16[640,384]{1,0:T(8,128)(2,1)S(1)}, bf16[640,384]{1,0:T(8,128)(2,1)S(1)}, u32[]{:S(2)}, u32[]{:S(2)}) collective-permute-start(bf16[640,384]{1,0:T(8,128)(2,1)S(1)} %pad_maximum_fusion.3), channel_id=1, source_target_pairs={{0,6},{1,3},{2,4},{3,1},{4,2},{5,7},{6,0},{7,5},{8,14},{9,11},{10,... | collective-permute-start | bytes 1474568 | tf_op jit(solution)/shard_map/ppermute | solution.py:64
  104.2 4.2 %collective-permute-start.21 = (f32[320,320]{1,0:T(8,128)S(1)}, f32[320,320]{1,0:T(8,128)S(1)}, u32[]{:S(2)}, u32[]{:S(2)}) collective-permute-start(f32[320,320]{1,0:T(8,128)S(1)} %fusion.6), channel_id=1, source_target_pairs={{0,1},{1,0},{2,3},{3,2},{4,5},{5,4},{6,7},{7,6},{8,9},{9,8},{10,11... | collective-permute-start | bytes 1228808 | tf_op jit(solution)/shard_map/ppermute | solution.py:64
  106.2 37.4 %collective-permute-start.13 = (bf16[320,1728]{1,0:T(8,128)(2,1)S(1)}, bf16[320,1728]{1,0:T(8,128)(2,1)S(1)}, u32[]{:S(2)}, u32[]{:S(2)}) collective-permute-start(bf16[320,1728]{1,0:T(8,128)(2,1)S(1)} %collective-permute-done.12), channel_id=1, source_target_pairs={{0,8},{1,57},{2,10},{3,59},{4,12},{5,61},{6,14},{7,63},{8,0},{9,17... | collective-permute-start | bytes 3317768 | tf_op jit(solution)/shard_map/ppermute | solution.py:64
  109.3 10.8 %collective-permute-start.22 = (f32[160,320]{1,0:T(8,128)S(1)}, f32[160,320]{1,0:T(8,128)S(1)}, u32[]{:S(2)}, u32[]{:S(2)}) collective-permute-start(f32[160,320]{1,0:T(8,128)S(1)} %pad_maximum_fusion.7), channel_id=1, source_target_pairs={{0,6},{1,3},{2,4},{3,1},{4,2},{5,7},{6,0},{7,5},{8,14},{9,11},{10,... | collective-permute-start | bytes 614408 | tf_op jit(solution)/shard_map/ppermute | solution.py:64
  120.1 11.1 %collective-permute-start.23 = (f32[80,320]{1,0:T(8,128)S(1)}, f32[80,320]{1,0:T(8,128)S(1)}, u32[]{:S(2)}, u32[]{:S(2)}) collective-permute-start(f32[80,320]{1,0:T(8,128)S(1)} %slice_add_fusion.1), channel_id=1, source_target_pairs={{0,2},{1,7},{2,0},{3,5},{4,6},{5,3},{6,4},{7,1},{8,10},{9,15},{10,... | collective-permute-start | bytes 307208 | tf_op jit(solution)/shard_map/ppermute | solution.py:64
  127.2 20.8 %collective-permute-start.7 = (bf16[1280,384]{1,0:T(8,128)(2,1)S(1)}, bf16[1280,384]{1,0:T(8,128)(2,1)S(1)}, u32[]{:S(2)}, u32[]{:S(2)}) collective-permute-start(bf16[1280,384]{1,0:T(8,128)(2,1)S(1)} %bitcast.168), channel_id=1, source_target_pairs={{0,1},{1,0},{2,3},{3,2},{4,5},{5,4},{6,7},{7,6},{8,9},{9,8},{10,11... | collective-permute-start | bytes 2949128 | tf_op jit(solution)/shard_map/ppermute | solution.py:64
  131.3 10.3 %collective-permute-start.24 = (bf16[80,320]{1,0:T(8,128)(2,1)S(1)}, bf16[80,320]{1,0:T(8,128)(2,1)S(1)}, u32[]{:S(2)}, u32[]{:S(2)}) collective-permute-start(bf16[80,320]{1,0:T(8,128)(2,1)S(1)} %fusion.53), channel_id=1, source_target_pairs={{0,0},{1,64},{2,128},{3,192},{4,256},{5,320},{6,384},{7,448},{8,8}... | collective-permute-start | bytes 153608 | tf_op jit(solution)/shard_map/ppermute | solution.py:64
  141.6 24.5 %collective-permute-start.17 = (bf16[320,2432]{1,0:T(8,128)(2,1)S(1)}, bf16[320,2432]{1,0:T(8,128)(2,1)S(1)}, u32[]{:S(2)}, u32[]{:S(2)}) collective-permute-start(bf16[320,2432]{1,0:T(8,128)(2,1)S(1)} %collective-permute-done.15), channel_id=1, source_target_pairs={{0,384},{1,129},{2,386},{3,131},{4,388},{5,133},{6,390},{7,135},{8... | collective-permute-start | bytes 4669448 | tf_op jit(solution)/shard_map/ppermute | solution.py:64
  143.6 19.4 %collective-permute-start.14 = (bf16[320,1728]{1,0:T(8,128)(2,1)S(1)}, bf16[320,1728]{1,0:T(8,128)(2,1)S(1)}, u32[]{:S(2)}, u32[]{:S(2)}) collective-permute-start(bf16[320,1728]{1,0:T(8,128)(2,1)S(1)} %collective-permute-done.13), channel_id=1, source_target_pairs={{0,56},{1,9},{2,58},{3,11},{4,60},{5,13},{6,62},{7,15},{8,16},{9,1... | collective-permute-start | bytes 3317768 | tf_op jit(solution)/shard_map/ppermute | solution.py:64
  148.3 13.4 %collective-permute-start.25 = (bf16[1280,128]{1,0:T(8,128)(2,1)S(1)}, bf16[1280,128]{1,0:T(8,128)(2,1)S(1)}, u32[]{:S(2)}, u32[]{:S(2)}) collective-permute-start(bf16[1280,128]{1,0:T(8,128)(2,1)S(1)} %slice.173), channel_id=1, source_target_pairs={{0,64},{1,65},{2,66},{3,67},{4,68},{5,69},{6,70},{7,71},{8,72},{9,... | collective-permute-start | bytes 983048 | tf_op jit(solution)/shard_map/ppermute | solution.py:64
  166.5 7.9 %copy-start = (f32[216,1728]{1,0:T(8,128)S(1)}, f32[216,1728]{1,0:T(8,128)}, u32[]{:S(2)}) copy-start(f32[216,1728]{1,0:T(8,128)} %param.10) | copy-start | bytes 4478980
  166.5 11.0 %collective-permute-start.26 = (f32[80,640]{1,0:T(8,128)S(1)}, f32[80,640]{1,0:T(8,128)S(1)}, u32[]{:S(2)}, u32[]{:S(2)}) collective-permute-start(f32[80,640]{1,0:T(8,128)S(1)} %slice.179), channel_id=1, source_target_pairs={{0,64},{1,65},{2,66},{3,67},{4,68},{5,69},{6,70},{7,71},{8,72},{9,... | collective-permute-start | bytes 614408 | tf_op jit(solution)/shard_map/ppermute | solution.py:64
  174.5 3.1 %copy-start.2 = (f32[80,640]{1,0:T(8,128)S(1)}, f32[80,640]{1,0:T(8,128)}, u32[]{:S(2)}) copy-start(f32[80,640]{1,0:T(8,128)} %param.9) | copy-start | bytes 614404

commit v3 on v2

--- a/solution.py
+++ b/solution.py
@@ -53,7 +53,15 @@
 X_A, X_B = towards(X, 0), towards(X, 1)
 H_A, H_B = towards(ZH, 0), towards(ZH, 1)
 ZL_SWAP, C_SWAP = flipped(ZL), flipped(C)
+CROSS = tuple(
+    [p for p in pairs_of(move) if (p[0] // 64 + p[0]) % 2]
+    for move in (
+        lambda at: [at[X], 1 - at[ZL], at[Y], at[ZH], at[C]],
+        lambda at: [at[X], 1 - at[ZL], at[Y], at[ZH], 1 - at[C]],
+    )
+)
 TURN = pairs_of(lambda at: [at[ZH], at[C], at[Y], at[X], at[ZL]])
+TURN_H_A = [(i, TURN[j][1]) for i, j in H_A]
 
 
 def rows_major(x):
@@ -115,7 +123,8 @@
 
     def along_x(own):
         b1 = send(own, X_A)
-        b2 = send(jnp.concatenate([own, b1], 0), X_B)
+        pair = jnp.concatenate([own, b1], 0)
+        b2 = send(pair, X_B)
         m = own.shape[0]
         return placed((own, b1, b2[:m], b2[m:]), x_spots, 4)
 
@@ -147,31 +156,41 @@
     )
     h0 = send(part, TURN)
     h1 = send(h0, H_A)
-    h2 = send(jnp.concatenate([h0, h1], 0), H_B)
+
+    mine_g = by_y[:, wide_x : wide_x + wide_g]
+    half = contract_cols(w_keep, mine_g) + send(contract_cols(w_send, mine_g), C_SWAP)
+    half = half.reshape(4, feats, rows)
+    far = jnp.concatenate([row_of(half, (zh - dh) % 4), row_of(half, (zh - 2 * dh) % 4)], 0)
+    high = lax.reduce_precision(far, 8, 7)
+    far = jnp.concatenate([high, far - high], 0).astype(jnp.bfloat16)
+    far = jnp.pad(far, ((0, 0), (0, h0.shape[1] - rows)))
+    h2 = send(jnp.concatenate([h0, h1, far], 0), H_B)
+    far = h2[2 * rows :, :rows].astype(jnp.float32)
+    far = far[: 2 * feats] + far[2 * feats :]
+    here = row_of(half, zh) + far[:feats]
+    near = row_of(half, (zh + dh) % 4) + far[feats:]
+    here, near = send(here, TURN), send(near, TURN_H_A)
+    grad_input = (here + near).astype(jnp.bfloat16).T
+
     mine = placed(
-        (h0, h1, h2[:rows], h2[rows:]), [(zh + dh * k) % 4 for k in (0, 1, -1, -2)], 4
+        (h0, h1, h2[:rows], h2[rows : 2 * rows]),
+        [(zh + dh * k) % 4 for k in (0, 1, -1, -2)],
+        4,
     ).reshape(4 * rows, -1)
     theirs = send(mine, C_SWAP)
     n_own = jnp.where(own_core, mine, theirs)
     n_other = jnp.where(own_core, theirs, mine)
-    n_cross = send(n_other[:, :128], ZL_SWAP)
+    n_cross = jnp.where(own_core, send(mine[:, :128], CROSS[0]), send(mine[:, :128], CROSS[1]))
     n_fi = jnp.concatenate([n_own[:, :128], n_cross], 1).reshape(4, rows, 256)
     n_own = n_own.reshape(4, rows, -1)
 
-    mine_g = by_y[:, wide_x : wide_x + wide_g]
-    half = contract_cols(w_keep, mine_g) + send(contract_cols(w_send, mine_g), C_SWAP)
-    half = half.reshape(4, feats, rows)
-    far = jnp.concatenate([row_of(half, (zh - dh) % 4), row_of(half, (zh - 2 * dh) % 4)], 0)
-    far = send(far, H_B)
-    near = row_of(half, (zh + dh) % 4) + far[feats:]
-    grad_input = row_of(half, zh) + far[:feats] + send(near, H_A)
-    grad_input = send(grad_input.astype(jnp.bfloat16), TURN).T
-
     n_other = n_other.reshape(4, 8, n, -1).transpose(1, 0, 2, 3).reshape(4 * rows, -1)
-    total, fi_total = contract_rows(n_other, q_wide), 0.0
+    fi_total = 0.0
+    for piece, spot in zip(p_wide, x_spots):
+        fi_total = fi_total + contract_rows(row_of(n_fi, spot), piece[:, :wide_x])
+    total = contract_rows(n_other, q_wide)
     for piece, spot in zip(p_wide, x_spots):
         total = total + contract_rows(row_of(n_own, spot), piece[:, wide_x : wide_x + wide_g])
-        fi_total = fi_total + contract_rows(row_of(n_fi, spot), piece[:, :wide_x])
     grad_weight = total[:feats]
     new_factor_grad = keep * factor_grad + blend * total[128 : 128 + units]
     fi_got = send(fi_total[128 : 128 + feats], ZL_SWAP)

time: 181 us -> 184 us (1.017)
  waiting for transfers between devices: 58.5 us -> 64.2 us
  starting transfers between devices: 101 us -> 99.1 us
    ppermute x27, waiting for transfers between devices: 58.5 us -> 64.2 us  [send(): return rows_major(lax.ppermute(rows_major(x), AXES, pairs))]
    ppermute x27, starting transfers between devices: 101 us -> 99.1 us  [send(): return rows_major(lax.ppermute(rows_major(x), AXES, pairs))]
  transfers between devices with their start and end apart: 27 -> 27, of which waited for: 12 -> 12; matrix products, arithmetic and copies ran while one was open for 8% -> 9% of each run, Pallas kernels for 0% -> 0%
where the time goes in v3:
time: 184 us; the launch traced here: 183 us
  starting transfers between devices  99.1 us (54%)
  waiting for transfers between devices  64.2 us (35%)
  matrix products  8.88 us (5%)
  local copies, waits for them, and re-layouts  4.05 us (2%)
  other arithmetic  3.81 us (2%)
  between operations  2.56 us (1%)
    ppermute x27, starting transfers between devices, send(): return rows_major(lax.ppermute(rows_major(x), AXES, pairs))  99.1 us
    ppermute x27, waiting for transfers between devices, send(): return rows_major(lax.ppermute(rows_major(x), AXES, pairs))  64.2 us
    dot_general x9, matrix products, contract_rows(): lax.dot_general(left, right, (((0,), (0,)), ((), ())), preferred_element_...  7.33 us
  transfers between devices with their start and end apart: 27, of which 12 were waited for; matrix products, arithmetic and copies ran while one was open for 9% of the time, Pallas kernels for 0%

profile of v3, /device:TPU:6, one launch (start us, length us, event | category | flops | bytes accessed | tf_op | source)
XLA Modules:
  0.0 182.6 jit_solution(9739725977042453402)
XLA Ops:
  0.6 4.4 %collective-permute-start.6 = (bf16[80,1728]{1,0:T(8,128)(2,1)}, bf16[80,1728]{1,0:T(8,128)(2,1)S(1)}, u32[]{:S(2)}, u32[]{:S(2)}) collective-permute-start(bf16[80,1728]{1,0:T(8,128)(2,1)} %param.7), channel_id=1, source_target_pairs={{0,64},{1,65},{2,66},{3,67},{4,68},{5,69},{6,70},{7,71},{8,72},{9,... | collective-permute-start | bytes 829448 | tf_op jit(solution)/shard_map/ppermute | solution.py:72
  5.1 1.9 %collective-permute-start.12 = (bf16[40,1728]{1,0:T(8,128)(2,1)}, bf16[40,1728]{1,0:T(8,128)(2,1)S(1)}, u32[]{:S(2)}, u32[]{:S(2)}) collective-permute-start(bf16[40,1728]{1,0:T(8,128)(2,1)} %param.8), channel_id=1, source_target_pairs={{0,64},{1,65},{2,66},{3,67},{4,68},{5,69},{6,70},{7,71},{8,72},{9,... | collective-permute-start | bytes 414728 | tf_op jit(solution)/shard_map/ppermute | solution.py:72
  7.0 1.0 concatenate.35
  8.0 3.5 %collective-permute-start = (bf16[40,2432]{1,0:T(8,128)(2,1)S(1)}, bf16[40,2432]{1,0:T(8,128)(2,1)S(1)}, u32[]{:S(2)}, u32[]{:S(2)}) collective-permute-start(bf16[40,2432]{1,0:T(8,128)(2,1)S(1)} %concatenate.35), channel_id=1, source_target_pairs={{0,8},{1,57},{2,10},{3,59},{4,12},{5,61},{6,14},{7,63},{8,0},{9,17... | collective-permute-start | bytes 583688 | tf_op jit(solution)/shard_map/ppermute | solution.py:72
  12.8 2.4 %collective-permute-done.12 = bf16[40,1728]{1,0:T(8,128)(2,1)S(1)} collective-permute-done((bf16[40,1728]{1,0:T(8,128)(2,1)}, bf16[40,1728]{1,0:T(8,128)(2,1)S(1)}, u32[]{:S(2)}, u32[]{:S(2)}) %collective-permute-start.12) | collective-permute-done | bytes 138272 | tf_op jit(solution)/shard_map/ppermute | solution.py:72
  15.2 2.7 %collective-permute-start.13 = (bf16[40,1728]{1,0:T(8,128)(2,1)S(1)}, bf16[40,1728]{1,0:T(8,128)(2,1)S(1)}, u32[]{:S(2)}, u32[]{:S(2)}) collective-permute-start(bf16[40,1728]{1,0:T(8,128)(2,1)S(1)} %collective-permute-done.12), channel_id=1, source_target_pairs={{0,128},{1,385},{2,130},{3,387},{4,132},{5,389},{6,134},{7,391},{8... | collective-permute-start | bytes 414728 | tf_op jit(solution)/shard_map/ppermute | solution.py:72
  18.0 5.4 %collective-permute-start.1 = (bf16[80,2432]{1,0:T(8,128)(2,1)S(1)}, bf16[80,2432]{1,0:T(8,128)(2,1)S(1)}, u32[]{:S(2)}, u32[]{:S(2)}) collective-permute-start(bf16[80,2432]{1,0:T(8,128)(2,1)S(1)} %pad_maximum_fusion.4), channel_id=1, source_target_pairs={{0,56},{1,9},{2,58},{3,11},{4,60},{5,13},{6,62},{7,15},{8,16},{9,1... | collective-permute-start | bytes 1167368 | tf_op jit(solution)/shard_map/ppermute | solution.py:72
  23.5 3.1 %collective-permute-start.7 = (bf16[160,1728]{1,0:T(8,128)(2,1)S(1)}, bf16[160,1728]{1,0:T(8,128)(2,1)S(1)}, u32[]{:S(2)}, u32[]{:S(2)}) collective-permute-start(bf16[160,1728]{1,0:T(8,128)(2,1)S(1)} %constant_dynamic-update-slice_fusion), channel_id=1, source_target_pairs={{0,128},{1,385},{2,130},{3,387},{4,132},{5,389},{6,134},{7,391},{8... | collective-permute-start | bytes 1658888 | tf_op jit(solution)/shard_map/ppermute | solution.py:72
  26.8 2.4 %collective-permute-start.14 = (bf16[80,1728]{1,0:T(8,128)(2,1)S(1)}, bf16[80,1728]{1,0:T(8,128)(2,1)S(1)}, u32[]{:S(2)}, u32[]{:S(2)}) collective-permute-start(bf16[80,1728]{1,0:T(8,128)(2,1)S(1)} %pad_maximum_fusion.5), channel_id=1, source_target_pairs={{0,384},{1,129},{2,386},{3,131},{4,388},{5,133},{6,390},{7,135},{8... | collective-permute-start | bytes 829448 | tf_op jit(solution)/shard_map/ppermute | solution.py:72
  29.3 7.3 %collective-permute-done.14 = bf16[80,1728]{1,0:T(8,128)(2,1)S(1)} collective-permute-done((bf16[80,1728]{1,0:T(8,128)(2,1)S(1)}, bf16[80,1728]{1,0:T(8,128)(2,1)S(1)}, u32[]{:S(2)}, u32[]{:S(2)}) %collective-permute-start.14) | collective-permute-done | bytes 276512 | tf_op jit(solution)/shard_map/ppermute | solution.py:72
  36.6 1.9 %collective-permute-start.15 = (bf16[160,1728]{1,0:T(8,128)(2,1)S(1)}, bf16[160,1728]{1,0:T(8,128)(2,1)S(1)}, u32[]{:S(2)}, u32[]{:S(2)}) collective-permute-start(bf16[160,1728]{1,0:T(8,128)(2,1)S(1)} %bitcast.166), channel_id=1, source_target_pairs={{0,8},{1,57},{2,10},{3,59},{4,12},{5,61},{6,14},{7,63},{8,0},{9,17... | collective-permute-start | bytes 1658888 | tf_op jit(solution)/shard_map/ppermute | solution.py:72
  38.9 3.9 %collective-permute-start.2 = (bf16[80,2432]{1,0:T(8,128)(2,1)S(1)}, bf16[80,2432]{1,0:T(8,128)(2,1)S(1)}, u32[]{:S(2)}, u32[]{:S(2)}) collective-permute-start(bf16[80,2432]{1,0:T(8,128)(2,1)S(1)} %collective-permute-done.1), channel_id=1, source_target_pairs={{0,8},{1,57},{2,10},{3,59},{4,12},{5,61},{6,14},{7,63},{8,0},{9,17... | collective-permute-start | bytes 1167368 | tf_op jit(solution)/shard_map/ppermute | solution.py:72
  43.0 2.9 %collective-permute-start.8 = (bf16[320,1728]{1,0:T(8,128)(2,1)S(1)}, bf16[320,1728]{1,0:T(8,128)(2,1)S(1)}, u32[]{:S(2)}, u32[]{:S(2)}) collective-permute-start(bf16[320,1728]{1,0:T(8,128)(2,1)S(1)} %pad_maximum_fusion), channel_id=1, source_target_pairs={{0,384},{1,129},{2,386},{3,131},{4,388},{5,133},{6,390},{7,135},{8... | collective-permute-start | bytes 3317768 | tf_op jit(solution)/shard_map/ppermute | solution.py:72
  46.0 6.4 %collective-permute-done.2 = bf16[80,2432]{1,0:T(8,128)(2,1)S(1)} collective-permute-done((bf16[80,2432]{1,0:T(8,128)(2,1)S(1)}, bf16[80,2432]{1,0:T(8,128)(2,1)S(1)}, u32[]{:S(2)}, u32[]{:S(2)}) %collective-permute-start.2) | collective-permute-done | bytes 389152 | tf_op jit(solution)/shard_map/ppermute | solution.py:72
  52.4 3.4 %collective-permute-start.3 = (bf16[80,2432]{1,0:T(8,128)(2,1)S(1)}, bf16[80,2432]{1,0:T(8,128)(2,1)S(1)}, u32[]{:S(2)}, u32[]{:S(2)}) collective-permute-start(bf16[80,2432]{1,0:T(8,128)(2,1)S(1)} %collective-permute-done.2), channel_id=1, source_target_pairs={{0,56},{1,9},{2,58},{3,11},{4,60},{5,13},{6,62},{7,15},{8,16},{9,1... | collective-permute-start | bytes 1167368 | tf_op jit(solution)/shard_map/ppermute | solution.py:72
  56.0 3.6 %collective-permute-start.16 = (bf16[320,1728]{1,0:T(8,128)(2,1)S(1)}, bf16[320,1728]{1,0:T(8,128)(2,1)S(1)}, u32[]{:S(2)}, u32[]{:S(2)}) collective-permute-start(bf16[320,1728]{1,0:T(8,128)(2,1)S(1)} %pad_maximum_fusion.1), channel_id=1, source_target_pairs={{0,56},{1,9},{2,58},{3,11},{4,60},{5,13},{6,62},{7,15},{8,16},{9,1... | collective-permute-start | bytes 3317768 | tf_op jit(solution)/shard_map/ppermute | solution.py:72
  59.6 3.6 %collective-permute-done.3 = bf16[80,2432]{1,0:T(8,128)(2,1)S(1)} collective-permute-done((bf16[80,2432]{1,0:T(8,128)(2,1)S(1)}, bf16[80,2432]{1,0:T(8,128)(2,1)S(1)}, u32[]{:S(2)}, u32[]{:S(2)}) %collective-permute-start.3) | collective-permute-done | bytes 389152 | tf_op jit(solution)/shard_map/ppermute | solution.py:72
  63.6 10.5 %collective-permute-start.4 = (bf16[320,384]{1,0:T(8,128)(2,1)S(1)}, bf16[320,384]{1,0:T(8,128)(2,1)S(1)}, u32[]{:S(2)}, u32[]{:S(2)}) collective-permute-start(bf16[320,384]{1,0:T(8,128)(2,1)S(1)} %pad_maximum_fusion.6), channel_id=1, source_target_pairs={{0,0},{1,64},{2,128},{3,192},{4,256},{5,320},{6,384},{7,448},{8,8}... | collective-permute-start | bytes 737288 | tf_op jit(solution)/shard_map/ppermute | solution.py:72
  74.1 2.7 %collective-permute-start.19 = (bf16[320,2432]{1,0:T(8,128)(2,1)S(1)}, bf16[320,2432]{1,0:T(8,128)(2,1)S(1)}, u32[]{:S(2)}, u32[]{:S(2)}) collective-permute-start(bf16[320,2432]{1,0:T(8,128)(2,1)S(1)} %bitcast.153), channel_id=1, source_target_pairs={{0,128},{1,385},{2,130},{3,387},{4,132},{5,389},{6,134},{7,391},{8... | collective-permute-start | bytes 4669448 | tf_op jit(solution)/shard_map/ppermute | solution.py:72
  76.8 1.9 %collective-permute-start.20 = (bf16[320,2432]{1,0:T(8,128)(2,1)S(1)}, bf16[320,2432]{1,0:T(8,128)(2,1)S(1)}, u32[]{:S(2)}, u32[]{:S(2)}) collective-permute-start(bf16[320,2432]{1,0:T(8,128)(2,1)S(1)} %bitcast.154), channel_id=1, source_target_pairs={{0,384},{1,129},{2,386},{3,131},{4,388},{5,133},{6,390},{7,135},{8... | collective-permute-start | bytes 4669448 | tf_op jit(solution)/shard_map/ppermute | solution.py:72
  78.8 11.5 %collective-permute-done.4 = bf16[320,384]{1,0:T(8,128)(2,1)S(1)} collective-permute-done((bf16[320,384]{1,0:T(8,128)(2,1)S(1)}, bf16[320,384]{1,0:T(8,128)(2,1)S(1)}, u32[]{:S(2)}, u32[]{:S(2)}) %collective-permute-start.4) | collective-permute-done | bytes 245792 | tf_op jit(solution)/shard_map/ppermute | solution.py:72
  90.3 1.9 %collective-permute-start.5 = (bf16[320,384]{1,0:T(8,128)(2,1)S(1)}, bf16[320,384]{1,0:T(8,128)(2,1)S(1)}, u32[]{:S(2)}, u32[]{:S(2)}) collective-permute-start(bf16[320,384]{1,0:T(8,128)(2,1)S(1)} %collective-permute-done.4), channel_id=1, source_target_pairs={{0,2},{1,7},{2,0},{3,5},{4,6},{5,3},{6,4},{7,1},{8,10},{9,15},{10,... | collective-permute-start | bytes 737288 | tf_op jit(solution)/shard_map/ppermute | solution.py:72
  92.5 0.8 fusion.8
  93.3 1.9 %collective-permute-start.9 = (f32[320,320]{1,0:T(8,128)S(1)}, f32[320,320]{1,0:T(8,128)S(1)}, u32[]{:S(2)}, u32[]{:S(2)}) collective-permute-start(f32[320,320]{1,0:T(8,128)S(1)} %fusion.8), channel_id=1, source_target_pairs={{0,1},{1,0},{2,3},{3,2},{4,5},{5,4},{6,7},{7,6},{8,9},{9,8},{10,11... | collective-permute-start | bytes 1228808 | tf_op jit(solution)/shard_map/ppermute | solution.py:72
  95.4 3.9 %collective-permute-done.5 = bf16[320,384]{1,0:T(8,128)(2,1)S(1)} collective-permute-done((bf16[320,384]{1,0:T(8,128)(2,1)S(1)}, bf16[320,384]{1,0:T(8,128)(2,1)S(1)}, u32[]{:S(2)}, u32[]{:S(2)}) %collective-permute-start.5) | collective-permute-done | bytes 245792 | tf_op jit(solution)/shard_map/ppermute | solution.py:72
  99.3 1.9 %collective-permute-start.17 = (bf16[320,1728]{1,0:T(8,128)(2,1)S(1)}, bf16[320,1728]{1,0:T(8,128)(2,1)S(1)}, u32[]{:S(2)}, u32[]{:S(2)}) collective-permute-start(bf16[320,1728]{1,0:T(8,128)(2,1)S(1)} %collective-permute-done.16), channel_id=1, source_target_pairs={{0,8},{1,57},{2,10},{3,59},{4,12},{5,61},{6,14},{7,63},{8,0},{9,17... | collective-permute-start | bytes 3317768 | tf_op jit(solution)/shard_map/ppermute | solution.py:72
  101.3 0.8 convolution_add_fusion.6
  102.3 4.1 %collective-permute-start.10 = (bf16[960,384]{1,0:T(8,128)(2,1)S(1)}, bf16[960,384]{1,0:T(8,128)(2,1)S(1)}, u32[]{:S(2)}, u32[]{:S(2)}) collective-permute-start(bf16[960,384]{1,0:T(8,128)(2,1)S(1)} %pad_maximum_fusion.2), channel_id=1, source_target_pairs={{0,6},{1,3},{2,4},{3,1},{4,2},{5,7},{6,0},{7,5},{8,14},{9,11},{10,... | collective-permute-start | bytes 2211848 | tf_op jit(solution)/shard_map/ppermute | solution.py:72
  106.4 5.4 %collective-permute-done.19 = bf16[320,2432]{1,0:T(8,128)(2,1)S(1)} collective-permute-done((bf16[320,2432]{1,0:T(8,128)(2,1)S(1)}, bf16[320,2432]{1,0:T(8,128)(2,1)S(1)}, u32[]{:S(2)}, u32[]{:S(2)}) %collective-permute-start.19) | collective-permute-done | bytes 1556512 | tf_op jit(solution)/shard_map/ppermute | solution.py:72
  111.8 8.3 %collective-permute-start.21 = (bf16[320,2432]{1,0:T(8,128)(2,1)S(1)}, bf16[320,2432]{1,0:T(8,128)(2,1)S(1)}, u32[]{:S(2)}, u32[]{:S(2)}) collective-permute-start(bf16[320,2432]{1,0:T(8,128)(2,1)S(1)} %collective-permute-done.19), channel_id=1, source_target_pairs={{0,384},{1,129},{2,386},{3,131},{4,388},{5,133},{6,390},{7,135},{8... | collective-permute-start | bytes 4669448 | tf_op jit(solution)/shard_map/ppermute | solution.py:72
  120.1 3.7 %collective-permute-done.10 = bf16[960,384]{1,0:T(8,128)(2,1)S(1)} collective-permute-done((bf16[960,384]{1,0:T(8,128)(2,1)S(1)}, bf16[960,384]{1,0:T(8,128)(2,1)S(1)}, u32[]{:S(2)}, u32[]{:S(2)}) %collective-permute-start.10) | collective-permute-done | bytes 737312 | tf_op jit(solution)/shard_map/ppermute | solution.py:72
  123.9 4.8 %collective-permute-start.22 = (f32[80,320]{1,0:T(8,128)S(1)}, f32[80,320]{1,0:T(8,128)S(1)}, u32[]{:S(2)}, u32[]{:S(2)}) collective-permute-start(f32[80,320]{1,0:T(8,128)S(1)} %get-tuple-element.9), channel_id=1, source_target_pairs={{0,0},{1,64},{2,128},{3,192},{4,256},{5,320},{6,384},{7,448},{8,8}... | collective-permute-start | bytes 307208 | tf_op jit(solution)/shard_map/ppermute | solution.py:72
  128.7 7.1 %collective-permute-start.23 = (f32[80,320]{1,0:T(8,128)S(1)}, f32[80,320]{1,0:T(8,128)S(1)}, u32[]{:S(2)}, u32[]{:S(2)}) collective-permute-start(f32[80,320]{1,0:T(8,128)S(1)} %get-tuple-element.8), channel_id=1, source_target_pairs={{0,128},{1,448},{2,0},{3,320},{4,384},{5,192},{6,256},{7,64},{8,13... | collective-permute-start | bytes 307208 | tf_op jit(solution)/shard_map/ppermute | solution.py:72
  136.0 5.9 %collective-permute-done.22 = f32[80,320]{1,0:T(8,128)S(1)} collective-permute-done((f32[80,320]{1,0:T(8,128)S(1)}, f32[80,320]{1,0:T(8,128)S(1)}, u32[]{:S(2)}, u32[]{:S(2)}) %collective-permute-start.22) | collective-permute-done | bytes 102432 | tf_op jit(solution)/shard_map/ppermute | solution.py:72
  141.9 1.3 collective-permute-start.24
  143.1 1.3 collective-permute-done.23
  145.8 5.6 %collective-permute-start.11 = (bf16[1280,384]{1,0:T(8,128)(2,1)S(1)}, bf16[1280,384]{1,0:T(8,128)(2,1)S(1)}, u32[]{:S(2)}, u32[]{:S(2)}) collective-permute-start(bf16[1280,384]{1,0:T(8,128)(2,1)S(1)} %bitcast.165), channel_id=1, source_target_pairs={{0,1},{1,0},{2,3},{3,2},{4,5},{5,4},{6,7},{7,6},{8,9},{9,8},{10,11... | collective-permute-start | bytes 2949128 | tf_op jit(solution)/shard_map/ppermute | solution.py:72
  151.5 3.5 %collective-permute-start.18 = (bf16[320,1728]{1,0:T(8,128)(2,1)S(1)}, bf16[320,1728]{1,0:T(8,128)(2,1)S(1)}, u32[]{:S(2)}, u32[]{:S(2)}) collective-permute-start(bf16[320,1728]{1,0:T(8,128)(2,1)S(1)} %collective-permute-done.17), channel_id=1, source_target_pairs={{0,56},{1,9},{2,58},{3,11},{4,60},{5,13},{6,62},{7,15},{8,16},{9,1... | collective-permute-start | bytes 3317768 | tf_op jit(solution)/shard_map/ppermute | solution.py:72
  156.8 0.9 fusion.6
  157.7 0.9 fusion.3
  158.6 11.8 %collective-permute-done.18 = bf16[320,1728]{1,0:T(8,128)(2,1)S(1)} collective-permute-done((bf16[320,1728]{1,0:T(8,128)(2,1)S(1)}, bf16[320,1728]{1,0:T(8,128)(2,1)S(1)}, u32[]{:S(2)}, u32[]{:S(2)}) %collective-permute-start.18) | collective-permute-done | bytes 1105952 | tf_op jit(solution)/shard_map/ppermute | solution.py:72
  170.6 2.1 %convolution_add_fusion.2 = f32[384,1728]{1,0:T(8,128)S(1)} fusion(f32[384,1728]{1,0:T(8,128)S(1)} %fusion.6, bf16[1280,384]{1,0:T(8,128)(2,1)S(1)} %bitcast.159, bf16[1280,1728]{1,0:T(8,128)(2,1)S(1)} %bitcast.150), kind=kOutput, calls=%fused_computation.3 | convolution fusion | flops 1699356672 | bytes 10715136 | tf_op jit(solution)/shard_map/dot_general | solution.py:77
  172.6 1.0 fusion
  174.1 3.7 %collective-permute-start.26 = (f32[80,640]{1,0:T(8,128)S(1)}, f32[80,640]{1,0:T(8,128)S(1)}, u32[]{:S(2)}, u32[]{:S(2)}) collective-permute-start(f32[80,640]{1,0:T(8,128)S(1)} %slice.195), channel_id=1, source_target_pairs={{0,64},{1,65},{2,66},{3,67},{4,68},{5,69},{6,70},{7,71},{8,72},{9,... | collective-permute-start | bytes 614408 | tf_op jit(solution)/shard_map/ppermute | solution.py:72
  177.7 0.9 convolution_add_fusion
  178.7 1.4 fusion.1
  180.1 0.8 slice.182
  180.9 0.9 collective-permute-done.26
  (86 shorter events, 6.8 us)
Async XLA Ops:
  0.6 12.1 %copy-start.1 = (bf16[80,1728]{1,0:T(8,128)(2,1)S(1)}, bf16[80,1728]{1,0:T(8,128)(2,1)}, u32[]{:S(2)}) copy-start(bf16[80,1728]{1,0:T(8,128)(2,1)} %param.7) | copy-start | bytes 829444
  0.6 22.8 %collective-permute-start.6 = (bf16[80,1728]{1,0:T(8,128)(2,1)}, bf16[80,1728]{1,0:T(8,128)(2,1)S(1)}, u32[]{:S(2)}, u32[]{:S(2)}) collective-permute-start(bf16[80,1728]{1,0:T(8,128)(2,1)} %param.7), channel_id=1, source_target_pairs={{0,64},{1,65},{2,66},{3,67},{4,68},{5,69},{6,70},{7,71},{8,72},{9,... | collective-permute-start | bytes 829448 | tf_op jit(solution)/shard_map/ppermute | solution.py:72
  5.1 10.1 %collective-permute-start.12 = (bf16[40,1728]{1,0:T(8,128)(2,1)}, bf16[40,1728]{1,0:T(8,128)(2,1)S(1)}, u32[]{:S(2)}, u32[]{:S(2)}) collective-permute-start(bf16[40,1728]{1,0:T(8,128)(2,1)} %param.8), channel_id=1, source_target_pairs={{0,64},{1,65},{2,66},{3,67},{4,68},{5,69},{6,70},{7,71},{8,72},{9,... | collective-permute-start | bytes 414728 | tf_op jit(solution)/shard_map/ppermute | solution.py:72
  8.0 9.9 %collective-permute-start = (bf16[40,2432]{1,0:T(8,128)(2,1)S(1)}, bf16[40,2432]{1,0:T(8,128)(2,1)S(1)}, u32[]{:S(2)}, u32[]{:S(2)}) collective-permute-start(bf16[40,2432]{1,0:T(8,128)(2,1)S(1)} %concatenate.35), channel_id=1, source_target_pairs={{0,8},{1,57},{2,10},{3,59},{4,12},{5,61},{6,14},{7,63},{8,0},{9,17... | collective-permute-start | bytes 583688 | tf_op jit(solution)/shard_map/ppermute | solution.py:72
  15.2 11.6 %collective-permute-start.13 = (bf16[40,1728]{1,0:T(8,128)(2,1)S(1)}, bf16[40,1728]{1,0:T(8,128)(2,1)S(1)}, u32[]{:S(2)}, u32[]{:S(2)}) collective-permute-start(bf16[40,1728]{1,0:T(8,128)(2,1)S(1)} %collective-permute-done.12), channel_id=1, source_target_pairs={{0,128},{1,385},{2,130},{3,387},{4,132},{5,389},{6,134},{7,391},{8... | collective-permute-start | bytes 414728 | tf_op jit(solution)/shard_map/ppermute | solution.py:72
  18.0 20.9 %collective-permute-start.1 = (bf16[80,2432]{1,0:T(8,128)(2,1)S(1)}, bf16[80,2432]{1,0:T(8,128)(2,1)S(1)}, u32[]{:S(2)}, u32[]{:S(2)}) collective-permute-start(bf16[80,2432]{1,0:T(8,128)(2,1)S(1)} %pad_maximum_fusion.4), channel_id=1, source_target_pairs={{0,56},{1,9},{2,58},{3,11},{4,60},{5,13},{6,62},{7,15},{8,16},{9,1... | collective-permute-start | bytes 1167368 | tf_op jit(solution)/shard_map/ppermute | solution.py:72
  23.5 19.5 %collective-permute-start.7 = (bf16[160,1728]{1,0:T(8,128)(2,1)S(1)}, bf16[160,1728]{1,0:T(8,128)(2,1)S(1)}, u32[]{:S(2)}, u32[]{:S(2)}) collective-permute-start(bf16[160,1728]{1,0:T(8,128)(2,1)S(1)} %constant_dynamic-update-slice_fusion), channel_id=1, source_target_pairs={{0,128},{1,385},{2,130},{3,387},{4,132},{5,389},{6,134},{7,391},{8... | collective-permute-start | bytes 1658888 | tf_op jit(solution)/shard_map/ppermute | solution.py:72
  26.8 9.7 %collective-permute-start.14 = (bf16[80,1728]{1,0:T(8,128)(2,1)S(1)}, bf16[80,1728]{1,0:T(8,128)(2,1)S(1)}, u32[]{:S(2)}, u32[]{:S(2)}) collective-permute-start(bf16[80,1728]{1,0:T(8,128)(2,1)S(1)} %pad_maximum_fusion.5), channel_id=1, source_target_pairs={{0,384},{1,129},{2,386},{3,131},{4,388},{5,133},{6,390},{7,135},{8... | collective-permute-start | bytes 829448 | tf_op jit(solution)/shard_map/ppermute | solution.py:72
  36.6 19.2 %collective-permute-start.15 = (bf16[160,1728]{1,0:T(8,128)(2,1)S(1)}, bf16[160,1728]{1,0:T(8,128)(2,1)S(1)}, u32[]{:S(2)}, u32[]{:S(2)}) collective-permute-start(bf16[160,1728]{1,0:T(8,128)(2,1)S(1)} %bitcast.166), channel_id=1, source_target_pairs={{0,8},{1,57},{2,10},{3,59},{4,12},{5,61},{6,14},{7,63},{8,0},{9,17... | collective-permute-start | bytes 1658888 | tf_op jit(solution)/shard_map/ppermute | solution.py:72
  38.9 13.5 %collective-permute-start.2 = (bf16[80,2432]{1,0:T(8,128)(2,1)S(1)}, bf16[80,2432]{1,0:T(8,128)(2,1)S(1)}, u32[]{:S(2)}, u32[]{:S(2)}) collective-permute-start(bf16[80,2432]{1,0:T(8,128)(2,1)S(1)} %collective-permute-done.1), channel_id=1, source_target_pairs={{0,8},{1,57},{2,10},{3,59},{4,12},{5,61},{6,14},{7,63},{8,0},{9,17... | collective-permute-start | bytes 1167368 | tf_op jit(solution)/shard_map/ppermute | solution.py:72
  43.0 49.2 %collective-permute-start.8 = (bf16[320,1728]{1,0:T(8,128)(2,1)S(1)}, bf16[320,1728]{1,0:T(8,128)(2,1)S(1)}, u32[]{:S(2)}, u32[]{:S(2)}) collective-permute-start(bf16[320,1728]{1,0:T(8,128)(2,1)S(1)} %pad_maximum_fusion), channel_id=1, source_target_pairs={{0,384},{1,129},{2,386},{3,131},{4,388},{5,133},{6,390},{7,135},{8... | collective-permute-start | bytes 3317768 | tf_op jit(solution)/shard_map/ppermute | solution.py:72
  52.4 10.8 %collective-permute-start.3 = (bf16[80,2432]{1,0:T(8,128)(2,1)S(1)}, bf16[80,2432]{1,0:T(8,128)(2,1)S(1)}, u32[]{:S(2)}, u32[]{:S(2)}) collective-permute-start(bf16[80,2432]{1,0:T(8,128)(2,1)S(1)} %collective-permute-done.2), channel_id=1, source_target_pairs={{0,56},{1,9},{2,58},{3,11},{4,60},{5,13},{6,62},{7,15},{8,16},{9,1... | collective-permute-start | bytes 1167368 | tf_op jit(solution)/shard_map/ppermute | solution.py:72
  56.0 43.3 %collective-permute-start.16 = (bf16[320,1728]{1,0:T(8,128)(2,1)S(1)}, bf16[320,1728]{1,0:T(8,128)(2,1)S(1)}, u32[]{:S(2)}, u32[]{:S(2)}) collective-permute-start(bf16[320,1728]{1,0:T(8,128)(2,1)S(1)} %pad_maximum_fusion.1), channel_id=1, source_target_pairs={{0,56},{1,9},{2,58},{3,11},{4,60},{5,13},{6,62},{7,15},{8,16},{9,1... | collective-permute-start | bytes 3317768 | tf_op jit(solution)/shard_map/ppermute | solution.py:72
  63.6 26.7 %collective-permute-start.4 = (bf16[320,384]{1,0:T(8,128)(2,1)S(1)}, bf16[320,384]{1,0:T(8,128)(2,1)S(1)}, u32[]{:S(2)}, u32[]{:S(2)}) collective-permute-start(bf16[320,384]{1,0:T(8,128)(2,1)S(1)} %pad_maximum_fusion.6), channel_id=1, source_target_pairs={{0,0},{1,64},{2,128},{3,192},{4,256},{5,320},{6,384},{7,448},{8,8}... | collective-permute-start | bytes 737288 | tf_op jit(solution)/shard_map/ppermute | solution.py:72
  74.1 37.7 %collective-permute-start.19 = (bf16[320,2432]{1,0:T(8,128)(2,1)S(1)}, bf16[320,2432]{1,0:T(8,128)(2,1)S(1)}, u32[]{:S(2)}, u32[]{:S(2)}) collective-permute-start(bf16[320,2432]{1,0:T(8,128)(2,1)S(1)} %bitcast.153), channel_id=1, source_target_pairs={{0,128},{1,385},{2,130},{3,387},{4,132},{5,389},{6,134},{7,391},{8... | collective-permute-start | bytes 4669448 | tf_op jit(solution)/shard_map/ppermute | solution.py:72
  76.8 79.5 %collective-permute-start.20 = (bf16[320,2432]{1,0:T(8,128)(2,1)S(1)}, bf16[320,2432]{1,0:T(8,128)(2,1)S(1)}, u32[]{:S(2)}, u32[]{:S(2)}) collective-permute-start(bf16[320,2432]{1,0:T(8,128)(2,1)S(1)} %bitcast.154), channel_id=1, source_target_pairs={{0,384},{1,129},{2,386},{3,131},{4,388},{5,133},{6,390},{7,135},{8... | collective-permute-start | bytes 4669448 | tf_op jit(solution)/shard_map/ppermute | solution.py:72
  90.3 9.0 %collective-permute-start.5 = (bf16[320,384]{1,0:T(8,128)(2,1)S(1)}, bf16[320,384]{1,0:T(8,128)(2,1)S(1)}, u32[]{:S(2)}, u32[]{:S(2)}) collective-permute-start(bf16[320,384]{1,0:T(8,128)(2,1)S(1)} %collective-permute-done.4), channel_id=1, source_target_pairs={{0,2},{1,7},{2,0},{3,5},{4,6},{5,3},{6,4},{7,1},{8,10},{9,15},{10,... | collective-permute-start | bytes 737288 | tf_op jit(solution)/shard_map/ppermute | solution.py:72
  93.3 8.0 %collective-permute-start.9 = (f32[320,320]{1,0:T(8,128)S(1)}, f32[320,320]{1,0:T(8,128)S(1)}, u32[]{:S(2)}, u32[]{:S(2)}) collective-permute-start(f32[320,320]{1,0:T(8,128)S(1)} %fusion.8), channel_id=1, source_target_pairs={{0,1},{1,0},{2,3},{3,2},{4,5},{5,4},{6,7},{7,6},{8,9},{9,8},{10,11... | collective-permute-start | bytes 1228808 | tf_op jit(solution)/shard_map/ppermute | solution.py:72
  99.3 46.5 %collective-permute-start.17 = (bf16[320,1728]{1,0:T(8,128)(2,1)S(1)}, bf16[320,1728]{1,0:T(8,128)(2,1)S(1)}, u32[]{:S(2)}, u32[]{:S(2)}) collective-permute-start(bf16[320,1728]{1,0:T(8,128)(2,1)S(1)} %collective-permute-done.16), channel_id=1, source_target_pairs={{0,8},{1,57},{2,10},{3,59},{4,12},{5,61},{6,14},{7,63},{8,0},{9,17... | collective-permute-start | bytes 3317768 | tf_op jit(solution)/shard_map/ppermute | solution.py:72
  102.3 21.5 %collective-permute-start.10 = (bf16[960,384]{1,0:T(8,128)(2,1)S(1)}, bf16[960,384]{1,0:T(8,128)(2,1)S(1)}, u32[]{:S(2)}, u32[]{:S(2)}) collective-permute-start(bf16[960,384]{1,0:T(8,128)(2,1)S(1)} %pad_maximum_fusion.2), channel_id=1, source_target_pairs={{0,6},{1,3},{2,4},{3,1},{4,2},{5,7},{6,0},{7,5},{8,14},{9,11},{10,... | collective-permute-start | bytes 2211848 | tf_op jit(solution)/shard_map/ppermute | solution.py:72
  111.8 61.8 %collective-permute-start.21 = (bf16[320,2432]{1,0:T(8,128)(2,1)S(1)}, bf16[320,2432]{1,0:T(8,128)(2,1)S(1)}, u32[]{:S(2)}, u32[]{:S(2)}) collective-permute-start(bf16[320,2432]{1,0:T(8,128)(2,1)S(1)} %collective-permute-done.19), channel_id=1, source_target_pairs={{0,384},{1,129},{2,386},{3,131},{4,388},{5,133},{6,390},{7,135},{8... | collective-permute-start | bytes 4669448 | tf_op jit(solution)/shard_map/ppermute | solution.py:72
  123.9 17.9 %collective-permute-start.22 = (f32[80,320]{1,0:T(8,128)S(1)}, f32[80,320]{1,0:T(8,128)S(1)}, u32[]{:S(2)}, u32[]{:S(2)}) collective-permute-start(f32[80,320]{1,0:T(8,128)S(1)} %get-tuple-element.9), channel_id=1, source_target_pairs={{0,0},{1,64},{2,128},{3,192},{4,256},{5,320},{6,384},{7,448},{8,8}... | collective-permute-start | bytes 307208 | tf_op jit(solution)/shard_map/ppermute | solution.py:72
  128.7 15.8 %collective-permute-start.23 = (f32[80,320]{1,0:T(8,128)S(1)}, f32[80,320]{1,0:T(8,128)S(1)}, u32[]{:S(2)}, u32[]{:S(2)}) collective-permute-start(f32[80,320]{1,0:T(8,128)S(1)} %get-tuple-element.8), channel_id=1, source_target_pairs={{0,128},{1,448},{2,0},{3,320},{4,384},{5,192},{6,256},{7,64},{8,13... | collective-permute-start | bytes 307208 | tf_op jit(solution)/shard_map/ppermute | solution.py:72
  141.9 9.6 %collective-permute-start.24 = (bf16[1280,128]{1,0:T(8,128)(2,1)S(1)}, bf16[1280,128]{1,0:T(8,128)(2,1)S(1)}, u32[]{:S(2)}, u32[]{:S(2)}) collective-permute-start(bf16[1280,128]{1,0:T(8,128)(2,1)S(1)} %slice.189), channel_id=1, source_target_pairs={{1,65},{3,67},{5,69},{7,71},{9,73},{11,75},{13,77},{15,79},{17,81}... | collective-permute-start | bytes 983048 | tf_op jit(solution)/shard_map/ppermute | solution.py:72
  144.5 10.5 %collective-permute-start.25 = (bf16[1280,128]{1,0:T(8,128)(2,1)S(1)}, bf16[1280,128]{1,0:T(8,128)(2,1)S(1)}, u32[]{:S(2)}, u32[]{:S(2)}) collective-permute-start(bf16[1280,128]{1,0:T(8,128)(2,1)S(1)} %slice.189), channel_id=1, source_target_pairs={{1,64},{3,66},{5,68},{7,70},{9,72},{11,74},{13,76},{15,78},{17,80}... | collective-permute-start | bytes 983048 | tf_op jit(solution)/shard_map/ppermute | solution.py:72
  145.8 9.3 %collective-permute-start.11 = (bf16[1280,384]{1,0:T(8,128)(2,1)S(1)}, bf16[1280,384]{1,0:T(8,128)(2,1)S(1)}, u32[]{:S(2)}, u32[]{:S(2)}) collective-permute-start(bf16[1280,384]{1,0:T(8,128)(2,1)S(1)} %bitcast.165), channel_id=1, source_target_pairs={{0,1},{1,0},{2,3},{3,2},{4,5},{5,4},{6,7},{7,6},{8,9},{9,8},{10,11... | collective-permute-start | bytes 2949128 | tf_op jit(solution)/shard_map/ppermute | solution.py:72
  151.5 19.0 %collective-permute-start.18 = (bf16[320,1728]{1,0:T(8,128)(2,1)S(1)}, bf16[320,1728]{1,0:T(8,128)(2,1)S(1)}, u32[]{:S(2)}, u32[]{:S(2)}) collective-permute-start(bf16[320,1728]{1,0:T(8,128)(2,1)S(1)} %collective-permute-done.17), channel_id=1, source_target_pairs={{0,56},{1,9},{2,58},{3,11},{4,60},{5,13},{6,62},{7,15},{8,16},{9,1... | collective-permute-start | bytes 3317768 | tf_op jit(solution)/shard_map/ppermute | solution.py:72
  174.1 4.6 %copy-start = (f32[216,1728]{1,0:T(8,128)S(1)}, f32[216,1728]{1,0:T(8,128)}, u32[]{:S(2)}) copy-start(f32[216,1728]{1,0:T(8,128)} %param.10) | copy-start | bytes 4478980
  174.1 7.8 %collective-permute-start.26 = (f32[80,640]{1,0:T(8,128)S(1)}, f32[80,640]{1,0:T(8,128)S(1)}, u32[]{:S(2)}, u32[]{:S(2)}) collective-permute-start(f32[80,640]{1,0:T(8,128)S(1)} %slice.195), channel_id=1, source_target_pairs={{0,64},{1,65},{2,66},{3,67},{4,68},{5,69},{6,70},{7,71},{8,72},{9,... | collective-permute-start | bytes 614408 | tf_op jit(solution)/shard_map/ppermute | solution.py:72
  178.7 3.2 %copy-start.2 = (f32[80,640]{1,0:T(8,128)S(1)}, f32[80,640]{1,0:T(8,128)}, u32[]{:S(2)}) copy-start(f32[80,640]{1,0:T(8,128)} %param.9) | copy-start | bytes 614404
